TPU v7x, 32 devices: a whole 2x2x4 slice. The times are simulated.
32 devices in a mesh: dev: 32 (over z, y, x, core).
Axes of the slice: x: 2, y: 2, z: 4, core: 2. Of those that a mesh axis runs over, the one named last changes fastest.
Arguments:
- dual_blocks: bfloat16 [32, 3072, 3072], P('dev'), as said below
- rigid_modes: float32 [32, 6, 3072], P('dev'), may hold values from -5 to 5
- dual_local: float32 [32, 8, 3072], P('dev'), may hold values from -6 to 6
- coarse_rhs: float32 [32, 6, 8], P('dev'), may hold values from -4608 to 4608
- iface_sizes: int32 [32], P('dev'), may hold values from 1536 to 3072, as said below
- neighbours: int32 [32, 6], P('dev'), may hold values from -1 to 31, as said below
- shared_counts: int32 [32, 6], P('dev'), may hold values from 256 to 512, as said below
- iface_map: int32 [32, 3072], P('dev'), may hold values from -1 to 3071, as said below
- owner: int32 [32], replicated, may hold values from 0 to 31, as said below
Outputs:
- multipliers: float32 [32, 8, 3072], P('dev')
- projected_residual: float32 [32, 8, 3072], P('dev')
Inputs may be any that keep to these rules, and one draw needn't show every extreme that they name: `dual_blocks`: each block is symmetric positive definite, and so is each of its leading principal parts. Grid subdomain g is held by slot owner[g] = (g + s) mod 32 for one offset s of the draw, so the subdomains across the faces -x, +x, -y, +y, -z, +z of slot i sit in slots i - 1, i + 1, i - 4, i + 4, i - 16, i + 16, taken mod 32. `neighbours`: the subdomains form a grid of 4 x 4 x 32/16 with g = x + 4 y + 16 z. Row i lists, for the faces -x, +x, -y, +y, -z, +z of the subdomain held in slot i, the grid subdomain across that face, or -1 on the outer boundary; across a face from g the opposite face names g. `shared_counts`: equal on both sides of a shared face; some subdomain has 512 on all its faces. `iface_sizes`: the sum of the slot's shared_counts row; some subdomain has 3072. `iface_map`: for j < iface_sizes[i], entry j is f * 512 + p for the dof at position p of face f of slot i (p below that face's count), each such code once; -1 beyond. The dof at position p of a shared face pairs with the dof at position p of the opposite face of the neighbour.
All inputs are finite; a program needn't handle non-finite values.
Results may differ from a plain program's by a relative error of at most 0.025.
Values sent between devices are 32-bit elements; how exact they have to be, the bound alone decides.
A program may use at most 128 MiB of HBM per device.

v0:
```python
import functools

import jax
import jax.numpy as jnp
from jax import lax
from jax.experimental import pallas as pl
from jax.experimental.pallas import tpu as pltpu
from jax.sharding import PartitionSpec as P

FACES = 6
MODES = 6
ITERS = 3
LANES = 128
ROWS = 256
FACE_STEPS = (-1, 1, -4, 4, -16, 16)
HIGHEST = lax.Precision.HIGHEST


def params(steps=None):
    if steps is None:
        return pltpu.CompilerParams(vmem_limit_bytes=50 * 2**20)
    return pltpu.CompilerParams(
        dimension_semantics=("arbitrary",), vmem_limit_bytes=50 * 2**20
    )


def gather_lanes(source, index_ref, block):
    index = jnp.broadcast_to(index_ref[pl.ds(block, 1), :], (source.shape[0], LANES))
    low = jnp.bitwise_and(index, LANES - 1)
    high = jnp.right_shift(index, 7)
    picked = jnp.zeros((source.shape[0], LANES), jnp.float32)
    for part in range(source.shape[1] // LANES):
        taken = jnp.take_along_axis(
            source[:, part * LANES : (part + 1) * LANES], low, axis=1, mode="promise_in_bounds"
        )
        picked = jnp.where(high == part, taken, picked)
    return picked


def setup_kernel(codes_ref, values_ref, modes_ref, rhs_ref, inverse_ref, onehot_ref, left_ref):
    codes = codes_ref[...]
    nmax = codes.shape[1]
    blocks = nmax // LANES
    wide = left_ref.shape[0] // 3
    columns = lax.broadcasted_iota(jnp.int32, (1, nmax), 1)
    high = jnp.right_shift(codes, 7)
    low = jnp.where(codes < 0, -1, jnp.bitwise_and(codes, LANES - 1))
    rows = lax.broadcasted_iota(jnp.int32, (LANES, nmax), 0)
    onehot_ref[...] = jnp.where(rows == low, 1.0, 0.0).astype(jnp.bfloat16)
    hit = lax.broadcasted_iota(jnp.int32, (wide, nmax), 0) == high
    upper = jnp.right_shift(columns, 7).astype(jnp.float32)
    lower = jnp.bitwise_and(columns, LANES - 1).astype(jnp.float32)
    left_ref[:wide, :] = jnp.where(hit, upper, 0.0).astype(jnp.bfloat16)
    left_ref[wide : 2 * wide, :] = jnp.where(hit, lower, 0.0).astype(jnp.bfloat16)
    left_ref[2 * wide :, :] = jnp.where(hit, 1.0, 0.0).astype(jnp.bfloat16)
    found = lax.dot_general(
        left_ref[...], onehot_ref[...], (((1,), (1,)), ((), ())),
        preferred_element_type=jnp.float32,
    )
    place = found[:wide] * LANES + found[wide : 2 * wide]
    place = jnp.where(found[2 * wide :] > 0.5, place, float(nmax))
    inverse_ref[...] = (place[:blocks] + 0.5).astype(jnp.int32)

    def body(block, carry):
        start = pl.multiple_of(block * LANES, LANES)
        modes_ref[:, pl.ds(start, LANES)] = gather_lanes(values_ref.at[0], inverse_ref, block)
        rhs_ref[:, pl.ds(start, LANES)] = gather_lanes(values_ref.at[1], inverse_ref, block)
        return carry

    lax.fori_loop(0, blocks, body, 0)


def invert_kernel(matrix_ref, out_ref):
    size, width = out_ref.shape
    out_ref[...] = matrix_ref[...]
    lane = lax.broadcasted_iota(jnp.int32, (1, width), 1)

    def body(step, carry):
        k = 2 * step
        at0, at1 = lane == k, lane == k + 1
        row0 = out_ref[pl.ds(k, 1), :]
        row1 = out_ref[pl.ds(k + 1, 1), :]
        p00 = jnp.sum(jnp.where(at0, row0, 0.0), axis=1, keepdims=True)
        p01 = jnp.sum(jnp.where(at1, row0, 0.0), axis=1, keepdims=True)
        p11 = jnp.sum(jnp.where(at1, row1, 0.0), axis=1, keepdims=True)
        first = 1.0 / p00
        ratio = p01 * first
        i11 = 1.0 / (p11 - p01 * ratio)
        i01 = -ratio * i11
        i00 = first + ratio * ratio * i11
        use0 = i00 * row0 + i01 * row1
        use1 = i01 * row0 + i11 * row1
        whole = out_ref[...]
        col0 = jnp.sum(jnp.where(at0, whole, 0.0), axis=1, keepdims=True)
        col1 = jnp.sum(jnp.where(at1, whole, 0.0), axis=1, keepdims=True)
        fresh = whole - col0 * use0 - col1 * use1
        fresh = jnp.where(at0, col0 * i00 + col1 * i01, fresh)
        fresh = jnp.where(at1, col0 * i01 + col1 * i11, fresh)
        out_ref[...] = fresh
        out_ref[pl.ds(k, 1), :] = jnp.where(at0, -i00, jnp.where(at1, -i01, use0))
        out_ref[pl.ds(k + 1, 1), :] = jnp.where(at0, -i01, jnp.where(at1, -i11, use1))
        return carry

    lax.fori_loop(0, size // 2, body, 0)
    out_ref[...] = -out_ref[...]


def coarse_apply(coarse, picks_ref, modes_ref, far_ref, cap):
    z = lax.dot_general(
        coarse, picks_ref[...], (((1,), (0,)), ((), ())),
        precision=HIGHEST, preferred_element_type=jnp.float32,
    )
    blocks = []
    for face in range(FACES):
        span = slice(face * cap, (face + 1) * cap)
        total = jnp.zeros((coarse.shape[0], cap), jnp.float32)
        for mode in range(MODES):
            total += z[:, mode : mode + 1] * modes_ref[mode : mode + 1, span]
            column = (face + 1) * MODES + mode
            total -= z[:, column : column + 1] * far_ref[mode : mode + 1, span]
        blocks.append(total)
    return blocks


def product_steps(step, steps, vector_ref, map_ref, inverse_ref, dual_ref, sum_ref, outs, cap):
    per_step = dual_ref.shape[1] // LANES
    pieces = [gather_lanes(vector_ref, map_ref, step * per_step + i) for i in range(per_step)]
    vector = jnp.concatenate(pieces, axis=1).astype(jnp.bfloat16)
    part = jnp.dot(vector, dual_ref[0], preferred_element_type=jnp.float32)

    @pl.when(step == 0)
    def _():
        sum_ref[...] = part

    @pl.when(step > 0)
    def _():
        sum_ref[...] += part

    @pl.when(step == steps - 1)
    def _():
        def body(block, carry):
            start = pl.multiple_of(block * LANES, LANES)
            for face in range(FACES):
                outs[face][:, pl.ds(start, LANES)] = gather_lanes(
                    sum_ref, inverse_ref, face * (cap // LANES) + block
                )
            return carry

        lax.fori_loop(0, cap // LANES, body, 0)


def start_kernel(
    steps, cap, coarse_ref, picks_ref, modes_ref, far_ref, map_ref, inverse_ref, dual_ref,
    mult_ref, *rest,
):
    outs, sum_ref = rest[:FACES], rest[FACES]
    step = pl.program_id(0)

    @pl.when(step == 0)
    def _():
        parts = coarse_apply(coarse_ref[...], picks_ref, modes_ref, far_ref, cap)
        for face, part in enumerate(parts):
            mult_ref[:, face * cap : (face + 1) * cap] = part

    product_steps(step, steps, mult_ref, map_ref, inverse_ref, dual_ref, sum_ref, outs, cap)


def first_kernel(
    steps, cap, gathered_ref, picks_ref, modes_ref, far_ref, residual_ref, map_ref, inverse_ref,
    dual_ref, w_ref, *rest,
):
    outs, sum_ref = rest[:FACES], rest[FACES]
    step = pl.program_id(0)

    @pl.when(step == 0)
    def _():
        coarse = jnp.sum(gathered_ref[...], axis=0)
        parts = coarse_apply(coarse, picks_ref, modes_ref, far_ref, cap)
        for face, part in enumerate(parts):
            span = slice(face * cap, (face + 1) * cap)
            w_ref[:, span] = residual_ref[:, span] - part

    product_steps(step, steps, w_ref, map_ref, inverse_ref, dual_ref, sum_ref, outs, cap)


def advance(
    cap, slots, gathered_ref, picks_ref, modes_ref, far_ref, state, applied_ref, scalars_ref, outs
):
    mult_ref, w_ref, d_ref, q_ref, s_ref = state
    mult_out, w_out, d_out, q_out, s_out, scalars_out = outs
    coarse = jnp.sum(gathered_ref[...], axis=0)
    base = slots * MODES
    rho, wa, wq, da = (coarse[:, base + i : base + i + 1] for i in range(4))
    rho_old, dq_old = scalars_ref[:, 0:1], scalars_ref[:, 1:2]
    beta = rho / rho_old
    dq = wa + beta * (wq + da) + beta * beta * dq_old
    alpha = rho / dq
    parts = coarse_apply(coarse, picks_ref, modes_ref, far_ref, cap)
    for face, part in enumerate(parts):
        span = slice(face * cap, (face + 1) * cap)
        applied = applied_ref[:, span]
        d = w_ref[:, span] + beta * d_ref[:, span]
        s = applied - part + beta * s_ref[:, span]
        mult_out[:, span] = mult_ref[:, span] + alpha * d
        w_out[:, span] = w_ref[:, span] - alpha * s
        if d_out is not None:
            d_out[:, span] = d
            s_out[:, span] = s
            q_out[:, span] = applied + beta * q_ref[:, span]
    if scalars_out is not None:
        lane = lax.broadcasted_iota(jnp.int32, scalars_out.shape, 1)
        scalars_out[...] = jnp.where(lane == 0, rho, jnp.where(lane == 1, dq, 0.0))


def step_kernel(
    steps, cap, slots, gathered_ref, picks_ref, modes_ref, far_ref, m_ref, w_ref, d_ref, q_ref,
    s_ref, applied_ref, scalars_ref, map_ref, inverse_ref, dual_ref,
    m_out, w_out, d_out, q_out, s_out, scalars_out, *rest,
):
    outs, sum_ref = rest[:FACES], rest[FACES]
    step = pl.program_id(0)

    @pl.when(step == 0)
    def _():
        advance(
            cap, slots, gathered_ref, picks_ref, modes_ref, far_ref,
            (m_ref, w_ref, d_ref, q_ref, s_ref), applied_ref, scalars_ref,
            (m_out, w_out, d_out, q_out, s_out, scalars_out),
        )

    product_steps(step, steps, w_out, map_ref, inverse_ref, dual_ref, sum_ref, outs, cap)


def last_kernel(
    cap, slots, gathered_ref, picks_ref, modes_ref, far_ref, m_ref, w_ref, d_ref, q_ref, s_ref,
    applied_ref, scalars_ref, map_ref, m_out, w_out, m_tmp, w_tmp,
):
    advance(
        cap, slots, gathered_ref, picks_ref, modes_ref, far_ref,
        (m_ref, w_ref, d_ref, q_ref, s_ref), applied_ref, scalars_ref,
        (m_tmp, w_tmp, None, None, None, None),
    )

    def body(block, carry):
        start = pl.multiple_of(block * LANES, LANES)
        m_out[0, :, pl.ds(start, LANES)] = gather_lanes(m_tmp, map_ref, block)
        w_out[0, :, pl.ds(start, LANES)] = gather_lanes(w_tmp, map_ref, block)
        return carry

    lax.fori_loop(0, m_tmp.shape[1] // LANES, body, 0)


def greet(partners):
    barrier = pltpu.get_barrier_semaphore()
    for partner in partners:
        pl.semaphore_signal(
            barrier, inc=1, device_id=(partner,), device_id_type=pl.DeviceIdType.MESH
        )
    pl.semaphore_wait(barrier, len(partners))


def face_copies(pieces, land_ref, send_sem, recv_sem, slots):
    me = lax.axis_index("dev")
    targets = [lax.rem(me + by + slots, slots) for by in FACE_STEPS]
    greet(targets)
    copies = [
        pltpu.make_async_remote_copy(
            src_ref=pieces[face],
            dst_ref=land_ref.at[face ^ 1],
            send_sem=send_sem.at[face],
            recv_sem=recv_sem.at[face ^ 1],
            device_id=(targets[face],),
            device_id_type=pl.DeviceIdType.MESH,
        )
        for face in range(FACES)
    ]
    for copy in copies:
        copy.start()
    return copies


def exchange_kernel(slots, *refs):
    pieces, out_ref, (land_ref, send_sem, recv_sem) = refs[:FACES], refs[FACES], refs[FACES + 1 :]
    cap = land_ref.shape[2]
    for copy in face_copies(pieces, land_ref, send_sem, recv_sem, slots):
        copy.wait()
    for face in range(FACES):
        out_ref[:, face * cap : (face + 1) * cap] = land_ref[face]


def everyone_kernel(slots, total, own_ref, out_ref, land_ref, send_sem, recv_sem):
    me = lax.axis_index("dev")
    barrier = pltpu.get_barrier_semaphore()

    def signal(by, carry):
        pl.semaphore_signal(
            barrier, inc=1, device_id=(lax.rem(me + by, slots),),
            device_id_type=pl.DeviceIdType.MESH,
        )
        return carry

    lax.fori_loop(1, slots, signal, 0)
    pl.semaphore_wait(barrier, slots - 1)

    def copy(by):
        return pltpu.make_async_remote_copy(
            src_ref=own_ref,
            dst_ref=land_ref.at[me],
            send_sem=send_sem.at[by],
            recv_sem=recv_sem.at[by],
            device_id=(lax.rem(me + by, slots),),
            device_id_type=pl.DeviceIdType.MESH,
        )

    def start(by, carry):
        copy(by).start()
        return carry

    def finish(by, carry):
        copy(by).wait()
        return carry

    lax.fori_loop(1, slots, start, 0)
    land_ref[me] = own_ref[...]
    lax.fori_loop(1, slots, finish, 0)
    if total:
        out_ref[0] = jnp.sum(land_ref[...], axis=0)
    else:
        out_ref[...] = land_ref[...]


def combine_kernel(cap, slots, initial, slot_ref, modes_ref, masks_ref, *rest):
    own, rest = rest[:FACES], rest[FACES:]
    rest, (far, send_sem, recv_sem) = rest[:-3], rest[-3:]
    if initial:
        rhs_ref, rhs_far_ref, out_ref, sums_ref = rest
    else:
        w_ref, d_ref, q_ref, out_ref, sums_ref = rest
    loads = own[0].shape[0]
    counts = MODES if initial else MODES + 4
    totals = [jnp.zeros((loads, cap), jnp.float32) for _ in range(counts)]
    for copy in face_copies(own, far, send_sem, recv_sem, slots):
        copy.wait()
    for face in range(FACES):
        span = slice(face * cap, (face + 1) * cap)
        shared = masks_ref[0:1, span]
        value = own[face][...] - shared * far[face]
        if initial:
            value = rhs_ref[:, span] - shared * rhs_far_ref[:, span] - value
        out_ref[:, span] = value
        for mode in range(MODES):
            totals[mode] += value * modes_ref[mode : mode + 1, span]
        if not initial:
            weights = masks_ref[1:2, span]
            weighted_w = weights * w_ref[:, span]
            totals[MODES] += weighted_w * w_ref[:, span]
            totals[MODES + 1] += weighted_w * value
            totals[MODES + 2] += weighted_w * q_ref[:, span]
            totals[MODES + 3] += weights * d_ref[:, span] * value
    lane = lax.broadcasted_iota(jnp.int32, sums_ref.shape, 1)
    result = jnp.zeros(sums_ref.shape, jnp.float32)
    for index, total in enumerate(totals):
        place = slot_ref[0] * MODES + index if index < MODES else slots * MODES + index - MODES
        result = jnp.where(lane == place, jnp.sum(total, axis=1, keepdims=True), result)
    sums_ref[...] = result


def per_device(
    dual_blocks, rigid_modes, dual_local, coarse_rhs, iface_sizes, neighbours, shared_counts,
    iface_map, owner,
):
    my_slot = lax.axis_index("dev")
    slots = lax.axis_size("dev")
    loads, nmax = dual_local.shape[1:]
    cap = nmax // FACES
    blocks = nmax // LANES
    size = slots * MODES
    width = -(-(size + 4) // LANES) * LANES
    steps = nmax // ROWS
    f32 = jnp.float32
    shape = jax.ShapeDtypeStruct
    vector, face_vec = shape((loads, nmax), f32), shape((loads, cap), f32)
    scalar_shape, sums_shape = shape((loads, LANES), f32), shape((loads, width), f32)

    live = jnp.arange(nmax, dtype=jnp.int32) < iface_sizes[0]
    codes = jnp.where(live, iface_map[0], -1)
    code_table = codes.reshape(blocks, LANES)
    padded = jnp.pad(rigid_modes[0], ((0, loads - MODES), (0, 0)))
    modes, rhs, inverse = pl.pallas_call(
        setup_kernel,
        out_shape=(vector, vector, shape((blocks, LANES), jnp.int32)),
        scratch_shapes=[
            pltpu.VMEM((LANES, nmax), jnp.bfloat16),
            pltpu.VMEM((3 * 32, nmax), jnp.bfloat16),
        ],
        compiler_params=params(),
    )(codes.reshape(1, nmax), jnp.stack([padded, dual_local[0]]))

    def linked(name):
        return pltpu.CompilerParams(
            collective_id=name, has_side_effects=True, vmem_limit_bytes=50 * 2**20
        )

    def face_scratch(rows):
        return [
            pltpu.VMEM((FACES, rows, cap), f32),
            pltpu.SemaphoreType.DMA((FACES,)),
            pltpu.SemaphoreType.DMA((FACES,)),
        ]

    def everyone(block, total):
        return pl.pallas_call(
            functools.partial(everyone_kernel, slots, total),
            out_shape=shape((1 if total else slots,) + block.shape, f32),
            scratch_shapes=[
                pltpu.VMEM((slots,) + block.shape, f32),
                pltpu.SemaphoreType.DMA((slots,)),
                pltpu.SemaphoreType.DMA((slots,)),
            ],
            compiler_params=linked(0 if total else 4),
        )(block)

    both = jnp.concatenate([modes, rhs], axis=0)
    far_both = pl.pallas_call(
        functools.partial(exchange_kernel, slots),
        out_shape=shape((2 * loads, nmax), f32),
        scratch_shapes=face_scratch(2 * loads),
        compiler_params=linked(3),
    )(*[both[:, f * cap : (f + 1) * cap] for f in range(FACES)])
    position = jnp.arange(cap, dtype=jnp.int32)
    counted = position[None, :] < shared_counts[0][:, None]
    shared = (counted & (neighbours[0] >= 0)[:, None]).astype(f32).reshape(1, nmax)
    weights = counted.astype(f32).reshape(1, nmax) - 0.5 * shared
    masks = jnp.concatenate([shared, weights, jnp.zeros((6, nmax), f32)], axis=0)
    far_both = far_both * shared
    far_modes, far_rhs = far_both[:loads], far_both[loads:]

    own6 = modes[:MODES].reshape(MODES, FACES, cap)
    far6 = far_modes[:MODES].reshape(MODES, FACES, cap)
    diagonal = lax.dot_general(
        modes[:MODES], modes[:MODES], (((1,), (1,)), ((), ())), precision=HIGHEST
    )
    coupling = -jnp.einsum("afp,bfp->fab", own6, far6, precision=HIGHEST)
    ids = jnp.arange(slots, dtype=jnp.int32)
    row = jnp.where((ids == my_slot)[None, :, None], diagonal[:, None, :], 0.0)
    for face in range(FACES):
        target = (my_slot + FACE_STEPS[face]) % slots
        row += jnp.where((ids == target)[None, :, None], coupling[face][:, None, :], 0.0)
    row = row.reshape(MODES, size)
    row = jnp.concatenate(
        [row, jnp.pad(coarse_rhs[0], ((0, 0), (0, width - size - loads)))]
        if width - size >= loads
        else [row, jnp.pad(coarse_rhs[0], ((0, 0), (0, LANES - loads)))],
        axis=1,
    )
    everything = everyone(jnp.pad(row, ((0, loads - MODES), (0, 0))), False)
    everything = everything[:, :MODES].reshape(size, row.shape[1])
    goal = jnp.pad(everything[:, size : size + loads].T, ((0, 0), (0, width - size)))
    matrix = jnp.pad(everything[:, :size], ((0, 0), (0, width - size)))
    inverted = pl.pallas_call(
        invert_kernel,
        out_shape=shape((size, width), f32),
        compiler_params=params(),
    )(matrix)
    groups = [
        lax.dynamic_slice(inverted, (((my_slot + by) % slots) * MODES, 0), (MODES, width))
        for by in (0,) + FACE_STEPS
    ]
    picks = jnp.pad(
        jnp.concatenate(groups, axis=0), ((0, LANES - MODES * (FACES + 1)), (0, 0))
    ).T
    picks = jnp.where((jnp.arange(width) < size)[:, None], picks, 0.0)

    def whole(item):
        return pl.BlockSpec(item.shape, lambda i, rank=len(item.shape): (0,) * rank)

    def with_product(kernel, ins, outs, *static):
        out_shape = tuple(outs) + (face_vec,) * FACES
        return pl.pallas_call(
            functools.partial(kernel, steps, cap, *static),
            grid=(steps,),
            in_specs=[whole(x) for x in ins]
            + [pl.BlockSpec((1, ROWS, nmax), lambda i: (0, i, 0))],
            out_specs=tuple(whole(x) for x in out_shape),
            out_shape=out_shape,
            scratch_shapes=[pltpu.VMEM((loads, nmax), f32)],
            compiler_params=params(steps),
        )(*ins, dual_blocks)

    slot_array = my_slot.reshape(1).astype(jnp.int32)

    def combine(own, extra, initial):
        ins = (modes, masks, *own, *extra)
        value, sums = pl.pallas_call(
            functools.partial(combine_kernel, cap, slots, initial),
            in_specs=[pl.BlockSpec(memory_space=pltpu.SMEM)]
            + [pl.BlockSpec(memory_space=pltpu.VMEM)] * len(ins),
            out_shape=(vector, sums_shape),
            scratch_shapes=face_scratch(loads),
            compiler_params=linked(1 if initial else 2),
        )(slot_array, *ins)
        return value, everyone(sums, True)

    mult, *own = with_product(
        start_kernel, (goal, picks, modes, far_modes, code_table, inverse), (vector,)
    )
    residual, gathered = combine(own, (rhs, far_rhs), True)
    w, *own = with_product(
        first_kernel, (gathered, picks, modes, far_modes, residual, code_table, inverse), (vector,)
    )
    d = q = s = jnp.zeros((loads, nmax), f32)
    scalars = jnp.broadcast_to(
        jnp.where(jnp.arange(LANES) == 0, 1.0, 0.0).astype(f32), (loads, LANES)
    )
    for step in range(ITERS):
        applied, gathered = combine(own, (w, d, q), False)
        ins = (gathered, picks, modes, far_modes, mult, w, d, q, s, applied, scalars, code_table)
        if step < ITERS - 1:
            mult, w, d, q, s, scalars, *own = with_product(
                step_kernel, ins + (inverse,), (vector,) * 5 + (scalar_shape,), slots
            )
    return pl.pallas_call(
        functools.partial(last_kernel, cap, slots),
        out_shape=(shape((1, loads, nmax), f32),) * 2,
        scratch_shapes=[pltpu.VMEM((loads, nmax), f32)] * 2,
        compiler_params=params(),
    )(*ins)


def solution(mesh):
    return jax.shard_map(
        per_device,
        mesh=mesh,
        in_specs=(
            P("dev", None, None),
            P("dev", None, None),
            P("dev", None, None),
            P("dev", None, None),
            P("dev"),
            P("dev", None),
            P("dev", None),
            P("dev", None),
            P(),
        ),
        out_specs=(P("dev", None, None), P("dev", None, None)),
        check_vma=False,
    )
```

profile of v0, /device:TPU:0, one launch (start us, length us, event | category | flops | bytes accessed | tf_op | source)
XLA Modules:
  0.0 185.6 jit_solution(13408845716395316040)
XLA Ops:
  1.5 0.7 compare_bitcast_fusion
  2.2 0.1 pad.34.clone
  2.3 0.1 broadcast_in_dim.189
  2.5 0.1 broadcast_in_dim.225
  2.7 0.1 broadcast_in_dim.219
  2.9 0.1 broadcast_in_dim.213
  3.1 0.1 broadcast_in_dim.207
  3.3 0.1 broadcast_in_dim.201
  3.5 0.1 broadcast_in_dim.195
  3.6 0.7 copy.43
  4.3 0.7 fusion.2.map_ref
  5.0 0.7 compare_select_fusion.codes_ref
  5.7 0.7 subtract_bitcast_fusion
  6.5 0.7 fusion.1
  7.3 0.9 copy.42
  8.2 0.9 pad_maximum_fusion.values_ref
  9.1 3.5 %shard_map.95 = (f32[8,3072]{1,0:T(8,128)S(1)}, f32[8,3072]{1,0:T(8,128)S(1)}, s32[24,128]{1,0:T(8,128)S(1)}) custom-call(s32[1,3072]{1,0:T(1,128)S(1)} %compare_select_fusion.codes_ref, f32[2,8,3072]{2,1,0:T(8,128)S(1)} %pad_maximum_fusion.values_ref), custom_call_target="tpu_custom_call" | custom-call | tf_op jit(solution)/shard_map/pallas_call | solution.py:389
  12.6 0.3 fusion.4
  12.9 0.1 broadcast_in_dim.192
  13.1 10.5 %shard_map.96 = f32[16,3072]{1,0:T(8,128)S(1)} custom-call(f32[16,512]{1,0:T(8,128)S(1)} %get-tuple-element.114.refs_0_, f32[16,512]{1,0:T(8,128)S(1)} %get-tuple-element.113.refs_1_, f32[16,512]{1,0:T(8,128)S(1)} %get-tuple-element.112.refs_2_, f32[16,512]{1,0:T(8,128)S(1)} %get-tuple-element.111.refs_3_, f32[16,512]{1,0:T(8,128)S(1)} %get-tuple-element.110.refs_4_, ...), custom_call_target="tpu_custom_call" | custom-call | tf_op jit(solution)/shard_map/pallas_call | solution.py:424
  23.6 0.3 convolution_negate_fusion
  23.9 0.1 fusion.6
  24.0 0.1 broadcast_in_dim.199
  24.2 0.1 broadcast_in_dim.229
  24.3 0.1 broadcast_in_dim.223
  24.4 0.1 broadcast_in_dim.217
  24.5 0.1 broadcast_in_dim.211
  24.7 0.1 broadcast_in_dim.205
  24.9 9.2 %shard_map.97 = f32[32,8,256]{2,1,0:T(8,128)S(1)} custom-call(f32[8,256]{1,0:T(8,128)S(1)} %pad.26.own_ref), custom_call_target="tpu_custom_call" | custom-call | tf_op jit(solution)/shard_map/pallas_call | solution.py:412
  34.1 0.1 slice.90
  34.3 0.7 broadcast_select_fusion.matrix_ref
  34.9 16.5 %shard_map.98 = f32[192,256]{1,0:T(8,128)S(1)} custom-call(f32[192,256]{1,0:T(8,128)S(1)} %broadcast_select_fusion.matrix_ref), custom_call_target="tpu_custom_call" | custom-call | tf_op jit(solution)/shard_map/pallas_call | solution.py:460
  51.5 0.4 concatenate.15
  51.9 0.1 copy.34
  52.0 0.1 select_bitcast_fusion.picks_ref
  52.1 13.3 %shard_map.99 = (f32[8,3072]{1,0:T(8,128)S(1)}, f32[8,512]{1,0:T(8,128)S(1)}, f32[8,512]{1,0:T(8,128)S(1)}, f32[8,512]{1,0:T(8,128)S(1)}, f32[8,512]{1,0:T(8,128...) custom-call(f32[8,256]{1,0:T(8,128)S(1)} %pad.27.coarse_ref, f32[256,128]{1,0:T(8,128)S(1)} %select_bitcast_fusion.picks_ref, ...), custom_call_target="tpu_custom_call" | custom-call | tf_op jit(solution)/shard_map/pallas_call | solution.py:479
  65.4 9.1 %shard_map.100 = (f32[8,3072]{1,0:T(8,128)S(1)}, f32[8,256]{1,0:T(8,128)S(1)}) custom-call(s32[1]{0:T(128)} %bitcast.slot_ref, f32[8,3072]{1,0:T(8,128)S(1)} %get-tuple-element.51.modes_ref, f32[8,3072]{1,0:T(8,128)S(1)} %get-tuple-element.123.masks_ref, f32[8,512]{1,0:T(8,128)S(1)} %get-tuple-element.54.rest_0_, f32[8,512]{1,0:T(8,128)S(1)} %get-tuple-element.55.rest_1_, ...), custom_call_target="tpu_custom_call" | custom-call | tf_op jit(solution)/shard_map/pallas_call | solution.py:494
  74.5 10.5 %shard_map.101.gathered_ref = f32[1,8,256]{2,1,0:T(8,128)S(1)} custom-call(f32[8,256]{1,0:T(8,128)S(1)} %get-tuple-element.60.own_ref), custom_call_target="tpu_custom_call" | custom-call | tf_op jit(solution)/shard_map/pallas_call | solution.py:412
  85.0 13.3 %shard_map.102 = (f32[8,3072]{1,0:T(8,128)S(1)}, f32[8,512]{1,0:T(8,128)S(1)}, f32[8,512]{1,0:T(8,128)S(1)}, f32[8,512]{1,0:T(8,128)S(1)}, f32[8,512]{1,0:T(8,12...) custom-call(f32[1,8,256]{2,1,0:T(8,128)S(1)} %shard_map.101.gathered_ref, ...), custom_call_target="tpu_custom_call" | custom-call | tf_op jit(solution)/shard_map/pallas_call | solution.py:479
  98.3 8.2 %shard_map.103 = (f32[8,3072]{1,0:T(8,128)S(1)}, f32[8,256]{1,0:T(8,128)S(1)}) custom-call(s32[1]{0:T(128)} %bitcast.slot_ref, f32[8,3072]{1,0:T(8,128)S(1)} %get-tuple-element.51.modes_ref, f32[8,3072]{1,0:T(8,128)S(1)} %get-tuple-element.123.masks_ref, f32[8,512]{1,0:T(8,128)S(1)} %get-tuple-element.62.rest_0_, f32[8,512]{1,0:T(8,128)S(1)} %get-tuple-element.63.rest_1_, ...), custom_call_target="tpu_custom_call" | custom-call | tf_op jit(solution)/shard_map/pallas_call | solution.py:494
  106.6 10.6 %shard_map.104.gathered_ref = f32[1,8,256]{2,1,0:T(8,128)S(1)} custom-call(f32[8,256]{1,0:T(8,128)S(1)} %get-tuple-element.69.own_ref), custom_call_target="tpu_custom_call" | custom-call | tf_op jit(solution)/shard_map/pallas_call | solution.py:412
  117.2 13.3 %shard_map.105 = (f32[8,3072]{1,0:T(8,128)S(1)}, f32[8,3072]{1,0:T(8,128)S(1)}, f32[8,3072]{1,0:T(8,128)S(1)}, f32[8,3072]{1,0:T(8,128)S(1)}, f32[8,3072]{1,0:T(...) custom-call(f32[1,8,256]{2,1,0:T(8,128)S(1)} %shard_map.104.gathered, ...), custom_call_target="tpu_custom_call" | custom-call | tf_op jit(solution)/shard_map/pallas_call | solution.py:479
  130.5 8.2 %shard_map.106 = (f32[8,3072]{1,0:T(8,128)S(1)}, f32[8,256]{1,0:T(8,128)S(1)}) custom-call(s32[1]{0:T(128)} %bitcast.slot_ref, f32[8,3072]{1,0:T(8,128)S(1)} %get-tuple-element.51.modes_ref, f32[8,3072]{1,0:T(8,128)S(1)} %get-tuple-element.123.masks_ref, f32[8,512]{1,0:T(8,128)S(1)} %get-tuple-element.72.rest_0_, f32[8,512]{1,0:T(8,128)S(1)} %get-tuple-element.73.rest_1_, ...), custom_call_target="tpu_custom_call" | custom-call | tf_op jit(solution)/shard_map/pallas_call | solution.py:494
  138.8 10.6 %shard_map.107.gathered_ref = f32[1,8,256]{2,1,0:T(8,128)S(1)} custom-call(f32[8,256]{1,0:T(8,128)S(1)} %get-tuple-element.81.own_ref), custom_call_target="tpu_custom_call" | custom-call | tf_op jit(solution)/shard_map/pallas_call | solution.py:412
  149.4 13.3 %shard_map.108 = (f32[8,3072]{1,0:T(8,128)S(1)}, f32[8,3072]{1,0:T(8,128)S(1)}, f32[8,3072]{1,0:T(8,128)S(1)}, f32[8,3072]{1,0:T(8,128)S(1)}, f32[8,3072]{1,0:T(...) custom-call(f32[1,8,256]{2,1,0:T(8,128)S(1)} %shard_map.107.gathered, ...), custom_call_target="tpu_custom_call" | custom-call | tf_op jit(solution)/shard_map/pallas_call | solution.py:479
  162.7 8.2 %shard_map.109 = (f32[8,3072]{1,0:T(8,128)S(1)}, f32[8,256]{1,0:T(8,128)S(1)}) custom-call(s32[1]{0:T(128)} %bitcast.slot_ref, f32[8,3072]{1,0:T(8,128)S(1)} %get-tuple-element.51.modes_ref, f32[8,3072]{1,0:T(8,128)S(1)} %get-tuple-element.123.masks_ref, f32[8,512]{1,0:T(8,128)S(1)} %get-tuple-element.86.rest_0_, f32[8,512]{1,0:T(8,128)S(1)} %get-tuple-element.87.rest_1_, ...), custom_call_target="tpu_custom_call" | custom-call | tf_op jit(solution)/shard_map/pallas_call | solution.py:494
  170.9 10.6 %shard_map.110.gathered_ref = f32[1,8,256]{2,1,0:T(8,128)S(1)} custom-call(f32[8,256]{1,0:T(8,128)S(1)} %get-tuple-element.95.own_ref), custom_call_target="tpu_custom_call" | custom-call | tf_op jit(solution)/shard_map/pallas_call | solution.py:412
  181.5 4.0 %shard_map.111 = (f32[1,8,3072]{2,1,0:T(8,128)}, f32[1,8,3072]{2,1,0:T(8,128)}) custom-call(f32[1,8,256]{2,1,0:T(8,128)S(1)} %shard_map.110.gathered_ref, f32[256,128]{1,0:T(8,128)S(1)} %select_bitcast_fusion.picks_ref, f32[8,3072]{1,0:T(8,128)S(1)} %get-tuple-element.51.modes_ref, f32[8,3072]{1,0:T(8,128)S(1)} %get-tuple-element.101.far_ref, ...), custom_call_target="tpu_custom_call" | custom-call | tf_op jit(solution)/shard_map/pallas_call | solution.py:522
  (43 shorter events, 1.0 us)
where the time goes:
time: 186 us
  Pallas kernels  173 us (93%)
  other arithmetic  5.5 us (3%)
  local copies, waits for them, and re-layouts  4.71 us (3%)
    pallas_call x4, Pallas kernels, with_product(): pl.pallas_call(functools.partial(kernel, steps, cap, *static), grid=(step...  53.2 us
    pallas_call x5, Pallas kernels, everyone(): pl.pallas_call(functools.partial(everyone_kernel, slots, total), out_shap...  51.4 us
    pallas_call x4, Pallas kernels, combine(): pl.pallas_call(functools.partial(combine_kernel, cap, slots, initial), in...  33.8 us
    pallas_call x1, Pallas kernels, per_device(): pl.pallas_call(invert_kernel, out_shape=shape((size, width), f32), compil...  16.5 us
    pallas_call x1, Pallas kernels, per_device(): pl.pallas_call(functools.partial(exchange_kernel, slots), out_shape=shape...  10.5 us
    pallas_call x1, Pallas kernels, per_device(): pl.pallas_call(functools.partial(last_kernel, cap, slots), out_shape=(sha...  4.04 us

commit v1 on v0

v1 whole, which is shorter than its diff:
```python
import functools

import jax
import jax.numpy as jnp
from jax import lax
from jax.experimental import pallas as pl
from jax.experimental.pallas import tpu as pltpu
from jax.sharding import PartitionSpec as P

FACES = 6
MODES = 6
ITERS = 3
ROUNDS = ITERS + 1
LANES = 128
LOW = 256
ROWS = 8
FACE_STEPS = (-1, 1, -4, 4, -16, 16)
BLOCK_STEPS = (0,) + FACE_STEPS
HIGHEST = lax.Precision.HIGHEST
MESH = pl.DeviceIdType.MESH
NN = (((1,), (0,)), ((), ()))
NT = (((1,), (1,)), ((), ()))


def coarse_order(slots):
    apart = []
    for slot in range(slots):
        if all((slot + by) % slots not in apart for by in FACE_STEPS):
            apart.append(slot)
    rest = [slot for slot in range(slots) if slot not in apart]
    first = -(-(len(rest) * MODES + ROWS) // LANES) * LANES
    second = -(-len(apart) * MODES // LANES) * LANES
    return apart, rest, first, second


def high_dot(a, b, dims=NN):
    return lax.dot_general(
        a, b, dims, precision=HIGHEST, preferred_element_type=jnp.float32
    )


def split(value, parts):
    out = []
    for part in range(parts):
        piece = value.astype(jnp.bfloat16)
        out.append(piece)
        if part < parts - 1:
            value = value - piece.astype(jnp.float32)
    return out


def row_sum(value):
    return jnp.sum(value, axis=1, keepdims=True)


class Solver:
    def __init__(self, slots, loads, nmax, cap):
        self.slots, self.loads, self.nmax, self.cap = slots, loads, nmax, cap
        self.apart, self.rest, self.first, self.second = coarse_order(slots)
        self.width = self.first + self.second
        self.rhs_lane = len(self.rest) * MODES
        self.merged = 16 % slots == -16 % slots
        self.ports = FACES - 1 if self.merged else FACES
        self.highs = nmax // LOW

    def span(self, face):
        return slice(face * self.cap, (face + 1) * self.cap)

    def scratch(self):
        f32 = jnp.float32
        n, nmax, width, ports = self.slots, self.nmax, self.width, self.ports
        vector = (ROWS, nmax)
        return dict(
            dual=pltpu.VMEM((nmax, nmax), jnp.bfloat16),
            onehot=pltpu.VMEM((LOW, nmax), jnp.bfloat16),
            stack=pltpu.VMEM((3 * ROWS * self.highs, nmax), jnp.bfloat16),
            codes=pltpu.VMEM((1, nmax), jnp.int32),
            pad=pltpu.VMEM(vector, f32),
            modes=pltpu.VMEM(vector, f32),
            far=pltpu.VMEM(vector, f32),
            rhs=pltpu.VMEM(vector, f32),
            shared=pltpu.VMEM((1, nmax), f32),
            weights=pltpu.VMEM((1, nmax), f32),
            m=pltpu.VMEM(vector, f32),
            w=pltpu.VMEM(vector, f32),
            d=pltpu.VMEM(vector, f32),
            q=pltpu.VMEM(vector, f32),
            s=pltpu.VMEM(vector, f32),
            ydof=pltpu.VMEM(vector, f32),
            y=pltpu.VMEM((ROUNDS,) + vector, f32),
            zface=pltpu.VMEM((ROUNDS + 1, ROWS, self.cap), f32),
            fland=pltpu.VMEM((ROUNDS + 1, ports, ROWS, self.cap), f32),
            tsend=pltpu.VMEM((ROUNDS, ROWS, LANES), f32),
            tland=pltpu.VMEM((ROUNDS, n, ROWS, LANES), f32),
            qsend=pltpu.VMEM((ROWS, width), f32),
            qland=pltpu.VMEM((n, ROWS, width), f32),
            packed=pltpu.VMEM((width, width), f32),
            dense=pltpu.VMEM((self.first, self.first), f32),
            basis=pltpu.VMEM((n * ROWS, width), f32),
            picks=pltpu.VMEM((ROWS * (FACES + 1), n * ROWS), f32),
            dual_sem=pltpu.SemaphoreType.DMA((self.highs,)),
            fsend_sem=pltpu.SemaphoreType.DMA((ROUNDS + 1, ports)),
            frecv_sem=pltpu.SemaphoreType.DMA((ROUNDS + 1, ports)),
            tsend_sem=pltpu.SemaphoreType.DMA((ROUNDS,)),
            trecv_sem=pltpu.SemaphoreType.DMA((ROUNDS,)),
            qsend_sem=pltpu.SemaphoreType.DMA((1,)),
            qrecv_sem=pltpu.SemaphoreType.DMA((1,)),
        )


    def prepare_codes(self, sizes_ref, map_ref):
        x = self.x
        columns = lax.broadcasted_iota(jnp.int32, (1, self.nmax), 1)
        x.codes[...] = jnp.where(columns < sizes_ref[0], map_ref[...], -1)

        def body(block, carry):
            at = pl.ds(pl.multiple_of(block * LANES, LANES), LANES)
            codes = x.codes[:, at]
            low = jnp.where(codes < 0, -1, jnp.bitwise_and(codes, LOW - 1))
            rows = lax.broadcasted_iota(jnp.int32, (LOW, LANES), 0)
            x.onehot[:, at] = jnp.where(rows == low, 1.0, 0.0).astype(jnp.bfloat16)
            return carry

        lax.fori_loop(0, self.nmax // LANES, body, 0)

    def to_face(self, source, store, parts):
        x, rows = self.x, ROWS * self.highs

        def body(block, carry):
            at = pl.ds(pl.multiple_of(block * LOW, LOW), LOW)
            high = jnp.right_shift(x.codes[:, at], 8)
            for index, piece in enumerate(split(source[:, at], parts)):
                piece = piece.astype(jnp.float32)
                stacked = [jnp.where(high == h, piece, 0.0) for h in range(self.highs)]
                x.stack[index * rows : (index + 1) * rows, at] = jnp.concatenate(
                    stacked, axis=0
                ).astype(jnp.bfloat16)
            return carry

        lax.fori_loop(0, self.highs, body, 0)
        found = lax.dot_general(
            x.stack[: parts * rows, :], x.onehot[...], NT, preferred_element_type=jnp.float32
        )
        total = found[:rows]
        for index in range(1, parts):
            total = total + found[index * rows : (index + 1) * rows]
        for h in range(self.highs):
            store(h, total[h * ROWS : (h + 1) * ROWS])

    def to_dof(self, source, store, parts):
        x, rows = self.x, ROWS * self.highs
        pieces = [split(source[:, h * LOW : (h + 1) * LOW], parts) for h in range(self.highs)]
        stacked = jnp.concatenate(
            [pieces[h][index].astype(jnp.float32) for index in range(parts)
             for h in range(self.highs)], axis=0,
        ).astype(jnp.bfloat16)
        for block in range(self.highs):
            at = slice(block * LOW, (block + 1) * LOW)
            found = jnp.dot(stacked, x.onehot[:, at], preferred_element_type=jnp.float32)
            total = found[:rows]
            for index in range(1, parts):
                total = total + found[index * rows : (index + 1) * rows]
            high = jnp.right_shift(x.codes[:, at], 8)
            picked = jnp.zeros((ROWS, LOW), jnp.float32)
            for h in range(self.highs):
                picked = jnp.where(high == h, total[h * ROWS : (h + 1) * ROWS], picked)
            store(at, picked)


    def others(self, act):
        def body(by, carry):
            act(lax.rem(self.me + by, self.slots))
            return carry

        lax.fori_loop(1, self.slots, body, 0)

    def face_copies(self, phase, source):
        x = self.x
        copies = []
        for port in range(self.ports):
            merged = self.merged and port == self.ports - 1
            opposite = port if merged else port ^ 1
            target = lax.rem(self.me + FACE_STEPS[port] + self.slots, self.slots)
            copies.append(pltpu.make_async_remote_copy(
                src_ref=x.zface.at[phase] if merged else source(port),
                dst_ref=x.fland.at[phase, opposite],
                send_sem=x.fsend_sem.at[phase, port],
                recv_sem=x.frecv_sem.at[phase, opposite],
                device_id=(target,),
                device_id_type=MESH,
            ))
        return copies

    def start_faces(self, phase, ref):
        x = self.x
        if self.merged:
            lower, upper = self.span(FACES - 2), self.span(FACES - 1)
            x.zface[phase] = jnp.where(x.shared[:, lower] > 0.0, ref[:, lower], ref[:, upper])
        copies = self.face_copies(phase, lambda face: ref.at[:, self.span(face)])
        for copy in copies:
            copy.start()
        return copies

    def far_face(self, phase, face):
        return self.x.fland[phase, min(face, self.ports - 1)] * self.x.shared[:, self.span(face)]

    def all_copy(self, source, landing, send_sem, recv_sem, target):
        return pltpu.make_async_remote_copy(
            src_ref=source, dst_ref=landing, send_sem=send_sem, recv_sem=recv_sem,
            device_id=(target,), device_id_type=MESH,
        )

    def send_all(self, source, landing, send_sem, recv_sem):
        self.others(lambda target: self.all_copy(
            source, landing.at[self.me], send_sem, recv_sem, target
        ).start())

    def wait_all(self, landing, send_sem, recv_sem):
        part = landing.at[pl.ds(0, self.slots - 1)]
        target = lax.rem(self.me + 1, self.slots)
        whole = self.all_copy(part, part, send_sem, recv_sem, target)
        whole.wait_recv()
        whole.wait_send()


    def own_inverse(self, block):
        lane = lax.broadcasted_iota(jnp.int32, (1, LANES), 1)
        sub = lax.broadcasted_iota(jnp.int32, (ROWS, 1), 0)
        for k in range(MODES):
            here = lane == k
            row, column = block[k : k + 1, :], block[:, k : k + 1]
            scale = 1.0 / block[k : k + 1, k : k + 1]
            use = row * scale
            fresh = jnp.where(here, column * scale, block - column * use)
            block = jnp.where(sub == k, jnp.where(here, -scale, use), fresh)
        return -block

    def coarse_row(self, table_ref, rhs_row_ref):
        x, n = self.x, self.slots
        lane = lax.broadcasted_iota(jnp.int32, (1, LANES), 1)
        own = jnp.zeros((ROWS, LANES), jnp.float32)
        for b in range(MODES):
            own = jnp.where(lane == b, row_sum(x.modes[...] * x.modes[b : b + 1, :]), own)
        inverse = self.own_inverse(own)
        laneslot, lanemode = table_ref[0:1, :], table_ref[1:2, :]
        far = jnp.zeros((ROWS, self.width), jnp.float32)
        for face in range(FACES):
            span = self.span(face)
            there = laneslot == lax.rem(self.me + FACE_STEPS[face] + n, n)
            for b in range(MODES):
                value = row_sum(x.modes[:, span] * x.far[b : b + 1, span])
                far -= jnp.where(there & (lanemode == b), value, 0.0)
        here = laneslot == self.me
        scaled = jnp.zeros((ROWS, self.width), jnp.float32)
        plain = far
        for b in range(MODES):
            scaled += inverse[:, b : b + 1] * far[b : b + 1, :]
            at = here & (lanemode == b)
            scaled += jnp.where(at, inverse[:, b : b + 1], 0.0)
            plain += jnp.where(at, own[:, b : b + 1], 0.0)
        apart = sum((self.me == slot).astype(jnp.int32) for slot in self.apart)
        x.qsend[...] = jnp.where(apart > 0, scaled, plain) + rhs_row_ref[...]

    def eliminate(self):
        out = self.x.dense
        lane = lax.broadcasted_iota(jnp.int32, (1, self.first), 1)

        def body(step, carry):
            k = 2 * step
            at0, at1 = lane == k, lane == k + 1
            row0 = out[pl.ds(k, 1), :]
            row1 = out[pl.ds(k + 1, 1), :]
            p00 = row_sum(jnp.where(at0, row0, 0.0))
            p01 = row_sum(jnp.where(at1, row0, 0.0))
            p11 = row_sum(jnp.where(at1, row1, 0.0))
            first = 1.0 / p00
            ratio = p01 * first
            i11 = 1.0 / (p11 - p01 * ratio)
            i01 = -ratio * i11
            i00 = first + ratio * ratio * i11
            use0 = i00 * row0 + i01 * row1
            use1 = i01 * row0 + i11 * row1
            whole = out[...]
            col0 = row_sum(jnp.where(at0, whole, 0.0))
            col1 = row_sum(jnp.where(at1, whole, 0.0))
            fresh = whole - col0 * use0 - col1 * use1
            fresh = jnp.where(at0, col0 * i00 + col1 * i01, fresh)
            fresh = jnp.where(at1, col0 * i01 + col1 * i11, fresh)
            out[...] = fresh
            out[pl.ds(k, 1), :] = jnp.where(at0, -i00, jnp.where(at1, -i01, use0))
            out[pl.ds(k + 1, 1), :] = jnp.where(at0, -i01, jnp.where(at1, -i11, use1))
            return carry

        lax.fori_loop(0, len(self.rest) * MODES // 2, body, 0)

    def coarse_inverse(self, table_ref):
        x, n, first = self.x, self.slots, self.first
        x.packed[...] = jnp.zeros(x.packed.shape, jnp.float32)
        for start, group in ((0, self.rest), (first, self.apart)):
            for place, slot in enumerate(group):
                at = start + place * MODES
                x.packed[at : at + MODES, :] = x.qland[slot, :MODES, :]
        x.dense[...] = x.packed[:first, :first] - high_dot(
            x.packed[:first, first:], x.packed[first:, :first]
        )
        self.eliminate()
        laneslot, lanemode = table_ref[0:1, :], table_ref[1:2, :]
        lane = lax.broadcasted_iota(jnp.int32, (1, self.width), 1)
        sub = lax.broadcasted_iota(jnp.int32, (ROWS, 1), 0)
        for slot in range(n):
            unit = jnp.where((laneslot == slot) & (lanemode == sub), 1.0, 0.0)
            if slot in self.apart:
                unit -= jnp.where(lane < self.rhs_lane, x.qland[slot], 0.0)
            x.basis[slot * ROWS : (slot + 1) * ROWS, :] = unit
        chosen = jnp.concatenate([
            x.basis[pl.ds(pl.multiple_of(lax.rem(self.me + by + n, n) * ROWS, ROWS), ROWS), :]
            for by in BLOCK_STEPS
        ], axis=0)
        solved = jnp.concatenate([
            -high_dot(chosen[:, :first], x.dense[...]),
            high_dot(chosen[:, first:], x.packed[first:, first:]),
        ], axis=1)
        x.picks[...] = high_dot(solved, x.basis[...], NT)

    def columns(self, found, mask):
        return [
            [row_sum(found[g * ROWS + a : g * ROWS + a + 1, :] * mask) for a in range(MODES)]
            for g in range(FACES + 1)
        ]

    def rigid_part(self, z, face):
        x, span = self.x, self.span(face)
        total = jnp.zeros((ROWS, self.cap), jnp.float32)
        for a in range(MODES):
            total += z[0][a] * x.modes[a : a + 1, span]
            total -= z[face + 1][a] * x.far[a : a + 1, span]
        return total


    def product(self, vector, store):
        x = self.x
        wide = 512
        x.stack[:ROWS, :] = jnp.zeros((ROWS, self.nmax), jnp.bfloat16)

        def keep(at, block):
            x.stack[:ROWS, at] = block.astype(jnp.bfloat16)

        self.to_dof(vector, keep, 1)

        def body(block, carry):
            at = pl.ds(pl.multiple_of(block * wide, wide), wide)
            x.ydof[:, at] = jnp.dot(
                x.stack[:ROWS, :], x.dual[:, at], preferred_element_type=jnp.float32
            )
            return carry

        lax.fori_loop(0, self.nmax // wide, body, 0)
        self.to_face(x.ydof, store, 2)

    def contributions(self, ref, scalars):
        x = self.x
        lane = lax.broadcasted_iota(jnp.int32, (ROWS, LANES), 1)
        sub = lax.broadcasted_iota(jnp.int32, (ROWS, LANES), 0)
        out = jnp.zeros((ROWS, LANES), jnp.float32)
        for load in range(self.loads):
            own = jnp.zeros((ROWS, self.cap), jnp.float32)
            for face in range(FACES):
                span = self.span(face)
                row = ref[load : load + 1, span]
                own += x.modes[:, span] * row
                other = row_sum(x.far[:, span] * row)
                out = jnp.where(lane == load * ROWS + face + 1, -other, out)
            out = jnp.where(lane == load * ROWS, row_sum(own), out)
        if scalars:
            spread = jnp.zeros((ROWS, LANES), jnp.float32)
            for index, value in enumerate(scalars):
                spread = jnp.where(lane == sub * ROWS + index, value, spread)
            out = jnp.where(sub == MODES, jnp.sum(spread, axis=0, keepdims=True), out)
        return out

    def collect(self, phase):
        x, n = self.x, self.slots
        lane = lax.broadcasted_iota(jnp.int32, (ROWS, LANES), 1)
        sub = lax.broadcasted_iota(jnp.int32, (ROWS, LANES), 0)
        group = jnp.bitwise_and(lane, ROWS - 1)
        total = x.tland[phase, 0]
        for slot in range(1, n):
            total = total + x.tland[phase, slot]
        merged = []
        for slot in range(n):
            value = x.tland[phase, slot]
            for face in range(FACES):
                sender = (slot - FACE_STEPS[face]) % n
                value = jnp.where(group == face + 1, x.tland[phase, sender], value)
            merged.append(value)
        found = high_dot(x.picks[...], jnp.concatenate(merged, axis=0))
        z = self.columns(found, jnp.where(jnp.right_shift(lane, 3) == sub, 1.0, 0.0))
        sums = [
            row_sum(jnp.where(lane == sub * ROWS + i, total[MODES : MODES + 1, :], 0.0))
            for i in range(4)
        ]
        return z, sums

    def communicate(self, phase, ref, scalars):
        x = self.x
        copies = self.start_faces(phase + 1, ref)
        x.tsend[phase] = self.contributions(ref, scalars)
        landing = x.tland.at[phase]
        self.send_all(x.tsend.at[phase], landing, x.tsend_sem.at[phase], x.trecv_sem.at[phase])
        x.tland[phase, self.me] = x.tsend[phase]
        self.wait_all(landing, x.tsend_sem.at[phase], x.trecv_sem.at[phase])
        for copy in copies:
            copy.wait()


    def run(self, sizes_ref, neighbours_ref, counts_ref, map_ref, modes_ref, local_ref,
            rhs_row_ref, table_ref, dual_ref, mult_out, resid_out, x):
        self.x = x
        self.me = lax.axis_index("dev")
        n, f32 = self.slots, jnp.float32
        loads = []
        for block in range(self.highs):
            at = pl.ds(block * LOW, LOW)
            copy = pltpu.make_async_copy(
                dual_ref.at[0, at, :], x.dual.at[at, :], x.dual_sem.at[block]
            )
            copy.start()
            loads.append(copy)
        barrier = pltpu.get_barrier_semaphore()
        self.others(lambda target: pl.semaphore_signal(
            barrier, inc=1, device_id=(target,), device_id_type=MESH
        ))

        self.prepare_codes(sizes_ref, map_ref)
        place = lax.broadcasted_iota(jnp.int32, (1, self.cap), 1)
        for face in range(FACES):
            counted = jnp.where(place < counts_ref[0, face], 1.0, 0.0)
            both = jnp.where(neighbours_ref[0, face] >= 0, counted, jnp.zeros_like(counted))
            x.shared[:, self.span(face)] = both
            x.weights[:, self.span(face)] = counted - 0.5 * both
        x.pad[...] = jnp.zeros((ROWS, self.nmax), f32)
        x.pad[:MODES, :] = modes_ref[0]

        def keep(ref):
            def store(high, block):
                ref[:, high * LOW : (high + 1) * LOW] = block
            return store

        self.to_face(x.pad, keep(x.modes), 3)
        pl.semaphore_wait(barrier, n - 1)
        copies = self.start_faces(0, x.modes)
        self.to_face(local_ref.at[0], keep(x.rhs), 3)
        for copy in copies:
            copy.wait()
        for face in range(FACES):
            x.far[:, self.span(face)] = self.far_face(0, face)
        self.coarse_row(table_ref, rhs_row_ref)
        self.send_all(x.qsend, x.qland, x.qsend_sem.at[0], x.qrecv_sem.at[0])
        x.qland[self.me] = x.qsend[...]
        self.wait_all(x.qland, x.qsend_sem.at[0], x.qrecv_sem.at[0])
        self.coarse_inverse(table_ref)

        tile = self.rhs_lane // LANES * LANES
        goal = x.qland[:, :, tile : tile + LANES].reshape(n * ROWS, LANES)
        lane = lax.broadcasted_iota(jnp.int32, (ROWS, LANES), 1)
        sub = lax.broadcasted_iota(jnp.int32, (ROWS, LANES), 0)
        mask = jnp.where(lane == sub + (self.rhs_lane - tile), 1.0, 0.0)
        goal = jnp.where(lane[0:1] >= self.rhs_lane - tile, goal, 0.0)
        z = self.columns(high_dot(x.picks[...], goal), mask)
        for face in range(FACES):
            x.m[:, self.span(face)] = self.rigid_part(z, face)
        for copy in loads:
            copy.wait()

        def first_store(high, block):
            at = slice(high * LOW, (high + 1) * LOW)
            x.y[0, :, at] = x.rhs[:, at] - block

        self.product(x.m, first_store)
        self.communicate(0, x.y.at[0], None)
        z, _ = self.collect(0)
        for face in range(FACES):
            span = self.span(face)
            x.w[:, span] = x.y[0, :, span] - self.far_face(1, face) - self.rigid_part(z, face)

        for phase in range(1, ROUNDS):
            self.product(x.w, keep(x.y.at[phase]))
            w, y = x.w[...], x.y[phase]
            weighted = w * x.weights[...]
            zero = jnp.zeros((ROWS, 1), f32)
            scalars = [
                row_sum(weighted * w),
                row_sum(w * y),
                row_sum(weighted * x.q[...]) if phase > 1 else zero,
                row_sum(x.d[...] * y) if phase > 1 else zero,
            ]
            self.communicate(phase, x.y.at[phase], scalars)
            z, (rho, wa, wq, da) = self.collect(phase)
            if phase > 1:
                beta = rho / rho_old
                curve = wa + beta * (wq + da) + beta * beta * curve
            else:
                beta, curve = None, wa
            step = rho / curve
            rho_old = rho
            for face in range(FACES):
                span = self.span(face)
                applied = x.y[phase, :, span] - self.far_face(phase + 1, face)
                d, q, s = x.w[:, span], applied, applied - self.rigid_part(z, face)
                if phase > 1:
                    d += beta * x.d[:, span]
                    q += beta * x.q[:, span]
                    s += beta * x.s[:, span]
                x.m[:, span] += step * d
                x.w[:, span] -= step * s
                if phase < ITERS:
                    x.d[:, span], x.q[:, span], x.s[:, span] = d, q, s

        for ref, out in ((x.m, mult_out), (x.w, resid_out)):
            def put(at, block, out=out):
                out[0, :, at] = block
            self.to_dof(ref, put, 3)


class Refs:
    def __init__(self, names, refs):
        self.__dict__.update(zip(names, refs))


def per_device(
    dual_blocks, rigid_modes, dual_local, coarse_rhs, iface_sizes, neighbours, shared_counts,
    iface_map, owner,
):
    slots = lax.axis_size("dev")
    loads, nmax = dual_local.shape[1:]
    solver = Solver(slots, loads, nmax, nmax // FACES)
    scratch = solver.scratch()
    names = list(scratch)

    def kernel(*refs):
        solver.run(*refs[:11], Refs(names, refs[11:]))

    laneslot, lanemode = [-1] * solver.width, [-1] * solver.width
    for start, group in ((0, solver.rest), (solver.first, solver.apart)):
        for place, slot in enumerate(group):
            for mode in range(MODES):
                laneslot[start + place * MODES + mode] = slot
                lanemode[start + place * MODES + mode] = mode
    table = jnp.array([laneslot, lanemode] + [[0] * solver.width] * 6, jnp.int32)
    left = solver.rhs_lane
    rhs_row = jnp.pad(
        coarse_rhs[0], ((0, ROWS - MODES), (left, solver.width - left - loads))
    )
    vmem, smem = pl.BlockSpec(memory_space=pltpu.VMEM), pl.BlockSpec(memory_space=pltpu.SMEM)
    result = jax.ShapeDtypeStruct((1, loads, nmax), jnp.float32)
    return pl.pallas_call(
        kernel,
        out_shape=(result, result),
        in_specs=[smem] * 3 + [vmem] * 5 + [pl.BlockSpec(memory_space=pl.ANY)],
        out_specs=(vmem, vmem),
        scratch_shapes=list(scratch.values()),
        compiler_params=pltpu.CompilerParams(
            collective_id=0, has_side_effects=True, vmem_limit_bytes=58 * 2**20
        ),
    )(
        iface_sizes, neighbours, shared_counts, iface_map, rigid_modes, dual_local, rhs_row,
        table, dual_blocks,
    )


def solution(mesh):
    return jax.shard_map(
        per_device,
        mesh=mesh,
        in_specs=(
            P("dev", None, None),
            P("dev", None, None),
            P("dev", None, None),
            P("dev", None, None),
            P("dev"),
            P("dev", None),
            P("dev", None),
            P("dev", None),
            P(),
        ),
        out_specs=(P("dev", None, None), P("dev", None, None)),
        check_vma=False,
    )
```

time: 186 us -> 85.5 us (0.46)
  Pallas kernels: 173 us -> 77.9 us
  other arithmetic: 5.5 us -> 0 us
    pallas_call x17 -> x1, Pallas kernels: 173 us -> 77.9 us  [per_device(): pl.pallas_call(kernel, out_shape=(result, result), in_specs=[smem] * 3 +...]
    unnamed x6 -> x4, local copies, waits for them, and re-layouts: 1.7 us -> 5.31 us
    broadcast_in_dim x32 -> x0, local copies, waits for them, and re-layouts: 2.23 us -> none  [the longest x25 1.85 us: per_device(): jnp.where((ids == target)[None, :, None], coupling[face][:, None, :], 0.0)]
where the time goes in v1:
time: 85.5 us; the launch traced here: 85.2 us
  Pallas kernels  77.9 us (91%)
  local copies, waits for them, and re-layouts  5.98 us (7%)
  between operations  1.29 us (2%)
    pallas_call x1, Pallas kernels, per_device(): pl.pallas_call(kernel, out_shape=(result, result), in_specs=[smem] * 3 +...  77.9 us
    unnamed x4, local copies, waits for them, and re-layouts  5.31 us

profile of v1, /device:TPU:0, one launch (start us, length us, event | category | flops | bytes accessed | tf_op | source)
XLA Modules:
  0.0 85.2 jit_solution(4079642338189612260)
XLA Ops:
  1.3 0.7 copy.14
  2.0 0.7 pad.4.refs_6_
  2.6 1.5 %copy.11.refs_4_ = f32[1,6,3072]{2,1,0:T(8,128)} copy(f32[1,6,3072]{2,0,1:T(1,128)} %param.11) | data formatting | bytes 147456 | tf_op args[1]
  4.2 77.9 %shard_map.104 = (f32[1,8,3072]{2,1,0:T(8,128)}, f32[1,8,3072]{2,1,0:T(8,128)}) custom-call(s32[1]{0:T(128)S(6)} %copy.17.refs_0_, s32[1,6]{1,0:T(1,128)} %refs_1_.1, s32[1,6]{1,0:T(1,128)} %refs_2_.1, s32[1,3072]{1,0:T(1,128)} %refs_3_.1, f32[1,6,3072]{2,1,0:T(8,128)} %copy.11.refs_4_, f32[1,8,3072]{2,1,0:T(8,128)} %refs_5_.1, f32[8,256]{1,0:T(8,128)} %pad.4.refs_6_, ...), custom_call_target="tpu_custom_call" | custom-call | tf_op jit(solution)/shard_map/pallas_call | solution.py:556
  82.1 1.5 %copy.18 = f32[1,8,3072]{2,1,0:T(8,128)} copy(f32[1,8,3072]{2,1,0:T(8,128)} %get-tuple-element.4) | data formatting | bytes 196608
  83.7 1.5 %copy.19 = f32[1,8,3072]{2,1,0:T(8,128)} copy(f32[1,8,3072]{2,1,0:T(8,128)} %get-tuple-element.5) | data formatting | bytes 196608

commit v2 on v1

v2 whole, which is shorter than its diff:
```python
import functools

import jax
import jax.numpy as jnp
from jax import lax
from jax.experimental import pallas as pl
from jax.experimental.pallas import tpu as pltpu
from jax.sharding import PartitionSpec as P

FACES = 6
MODES = 6
ITERS = 3
ROUNDS = ITERS + 1
LANES = 128
HALF = 64
WIDE = 1536
LOW = 256
ROWS = 8
FACE_STEPS = (-1, 1, -4, 4, -16, 16)
BLOCK_STEPS = (0,) + FACE_STEPS
HIGHEST = lax.Precision.HIGHEST
MESH = pl.DeviceIdType.MESH
NN = (((1,), (0,)), ((), ()))
NT = (((1,), (1,)), ((), ()))


def coarse_order(slots):
    apart = []
    for slot in range(slots):
        if all((slot + by) % slots not in apart for by in FACE_STEPS):
            apart.append(slot)
    rest = [slot for slot in range(slots) if slot not in apart]
    first = -(-len(rest) * MODES // LANES) * LANES
    second = -(-len(apart) * MODES // LANES) * LANES
    return apart, rest, first, second


def high_dot(a, b, dims=NN):
    return lax.dot_general(
        a, b, dims, precision=HIGHEST, preferred_element_type=jnp.float32
    )


def split(value, parts):
    out = []
    for part in range(parts):
        piece = value.astype(jnp.bfloat16)
        out.append(piece)
        if part < parts - 1:
            value = value - piece.astype(jnp.float32)
    return out


def row_sum(value):
    return jnp.sum(value, axis=1, keepdims=True)


class Solver:
    def __init__(self, slots, loads, nmax, cap):
        self.slots, self.loads, self.nmax, self.cap = slots, loads, nmax, cap
        self.apart, self.rest, self.first, self.second = coarse_order(slots)
        self.width = self.first + self.second
        self.lane_of = {}
        for start, group in ((0, self.rest), (self.first, self.apart)):
            for place, slot in enumerate(group):
                self.lane_of[slot] = start + place * MODES
        self.merged = 16 % slots == -16 % slots
        self.ports = FACES - 1 if self.merged else FACES
        self.highs = nmax // LOW

    def span(self, face):
        return slice(face * self.cap, (face + 1) * self.cap)

    def scratch(self):
        f32 = jnp.float32
        n, nmax, width, ports = self.slots, self.nmax, self.width, self.ports
        vector = (ROWS, nmax)
        return dict(
            dual=pltpu.VMEM((nmax, nmax), jnp.bfloat16),
            onehot=pltpu.VMEM((LOW, nmax), jnp.bfloat16),
            stack=pltpu.VMEM((3 * ROWS * self.highs, nmax), jnp.bfloat16),
            codes=pltpu.VMEM((1, nmax), jnp.int32),
            places=pltpu.VMEM((1, nmax), jnp.int32),
            unhot=pltpu.VMEM((LOW, nmax), jnp.bfloat16),
            small=pltpu.VMEM((ROWS, LANES), f32),
            own=pltpu.VMEM((2, ROWS, LANES), f32),
            pad=pltpu.VMEM(vector, f32),
            modes=pltpu.VMEM(vector, f32),
            far=pltpu.VMEM(vector, f32),
            shared=pltpu.VMEM((1, nmax), f32),
            weights=pltpu.VMEM((1, nmax), f32),
            counted=pltpu.VMEM((1, nmax), f32),
            m=pltpu.VMEM(vector, f32),
            w=pltpu.VMEM(vector, f32),
            d=pltpu.VMEM(vector, f32),
            q=pltpu.VMEM(vector, f32),
            s=pltpu.VMEM(vector, f32),
            a=pltpu.VMEM(vector, f32),
            dofs=pltpu.VMEM(vector, f32),
            yfresh=pltpu.VMEM(vector, f32),
            yw=pltpu.VMEM(vector, f32),
            ys=pltpu.VMEM(vector, f32),
            yrigid=pltpu.VMEM((ROWS * (FACES + 1), nmax), f32),
            y=pltpu.VMEM((ROUNDS,) + vector, f32),
            zface=pltpu.VMEM((ROUNDS + 1, ROWS, self.cap), f32),
            fland=pltpu.VMEM((ROUNDS + 1, ports, ROWS, self.cap), f32),
            tsend=pltpu.VMEM((ROUNDS + 1, ROWS // 2, LANES), f32),
            tland=pltpu.VMEM((ROUNDS + 1, n, ROWS // 2, LANES), f32),
            merged=pltpu.VMEM((n * ROWS // 2, LANES), f32),
            qrows=pltpu.VMEM((n, ROWS, width), f32),
            packed=pltpu.VMEM((width, width), f32),
            dense=pltpu.VMEM((self.first, self.first), f32),
            basis=pltpu.VMEM((n * ROWS, width), f32),
            halves=pltpu.VMEM((2, n * ROWS // 2, width), f32),
            picks=pltpu.VMEM((2 * ROWS * (FACES + 1), n * ROWS // 2), f32),
            map=pltpu.VMEM((1, nmax), jnp.int32),
            raw=pltpu.VMEM((MODES, 1, nmax), f32),
            local=pltpu.VMEM((1, self.loads, nmax), f32),
            goal=pltpu.VMEM((MODES, 1, self.loads), f32),
            table=pltpu.VMEM((ROWS, width), jnp.int32),
            links=pltpu.SMEM((1, FACES), jnp.int32),
            counts=pltpu.SMEM((1, FACES), jnp.int32),
            in_sem=pltpu.SemaphoreType.DMA((7,)),
            dual_sem=pltpu.SemaphoreType.DMA((self.highs,)),
            fsend_sem=pltpu.SemaphoreType.DMA((ROUNDS + 1, ports)),
            frecv_sem=pltpu.SemaphoreType.DMA((ROUNDS + 1, ports)),
            tsend_sem=pltpu.SemaphoreType.DMA((ROUNDS + 1,)),
            trecv_sem=pltpu.SemaphoreType.DMA((ROUNDS + 1,)),
        )


    def spread_low(self, codes_ref, onehot_ref):
        def body(block, carry):
            at = pl.ds(pl.multiple_of(block * LANES, LANES), LANES)
            codes = codes_ref[:, at]
            low = jnp.where(codes < 0, -1, jnp.bitwise_and(codes, LOW - 1))
            rows = lax.broadcasted_iota(jnp.int32, (LOW, LANES), 0)
            onehot_ref[:, at] = jnp.where(rows == low, 1.0, 0.0).astype(jnp.bfloat16)
            return carry

        lax.fori_loop(0, self.nmax // LANES, body, 0)

    def scatter_modes(self):
        x, rows, parts = self.x, ROWS * self.highs, 3

        def body(block, carry):
            at = pl.ds(pl.multiple_of(block * LOW, LOW), LOW)
            high = jnp.right_shift(x.codes[:, at], 8)
            for index, piece in enumerate(split(x.pad[:, at], parts)):
                piece = piece.astype(jnp.float32)
                stacked = [jnp.where(high == h, piece, 0.0) for h in range(self.highs)]
                x.stack[index * rows : (index + 1) * rows, at] = jnp.concatenate(
                    stacked, axis=0
                ).astype(jnp.bfloat16)
            return carry

        lax.fori_loop(0, self.highs, body, 0)
        found = lax.dot_general(
            x.stack[...], x.onehot[...], NT, preferred_element_type=jnp.float32
        )
        total = found[:rows] + found[rows : 2 * rows] + found[2 * rows :]
        sub = lax.broadcasted_iota(jnp.int32, (ROWS, LOW), 0)
        for h in range(self.highs):
            at = slice(h * LOW, (h + 1) * LOW)
            block = total[h * ROWS : (h + 1) * ROWS]
            x.modes[:, at] = jnp.where(sub < MODES, block, 0.0)
            place = block[MODES : MODES + 1] * LOW + block[MODES + 1 : MODES + 2]
            place = (place + 0.5).astype(jnp.int32)
            x.places[:, at] = jnp.where(x.counted[:, at] > 0.0, place, -1)

    def reorder(self, source, codes_ref, onehot_ref, parts, store):
        rows = ROWS * self.highs
        pieces = [split(source[:, h * LOW : (h + 1) * LOW], parts) for h in range(self.highs)]
        stacked = jnp.concatenate(
            [pieces[h][index].astype(jnp.float32) for index in range(parts)
             for h in range(self.highs)], axis=0,
        ).astype(jnp.bfloat16)
        for block in range(self.highs):
            at = slice(block * LOW, (block + 1) * LOW)
            found = jnp.dot(stacked, onehot_ref[:, at], preferred_element_type=jnp.float32)
            total = found[:rows]
            for index in range(1, parts):
                total = total + found[index * rows : (index + 1) * rows]
            high = jnp.right_shift(codes_ref[:, at], 8)
            picked = jnp.zeros((ROWS, LOW), jnp.float32)
            for h in range(self.highs):
                picked = jnp.where(high == h, total[h * ROWS : (h + 1) * ROWS], picked)
            store(at, picked)

    def to_dof(self, source, parts, store):
        self.reorder(source, self.x.codes, self.x.onehot, parts, store)

    def to_face(self, source, parts, store):
        self.reorder(source, self.x.places, self.x.unhot, parts, store)


    def others(self, act):
        def body(by, carry):
            act(lax.rem(self.me + by, self.slots))
            return carry

        lax.fori_loop(1, self.slots, body, 0)

    def face_copies(self, phase, source):
        x = self.x
        copies = []
        for port in range(self.ports):
            merged = self.merged and port == self.ports - 1
            opposite = port if merged else port ^ 1
            target = lax.rem(self.me + FACE_STEPS[port] + self.slots, self.slots)
            copies.append(pltpu.make_async_remote_copy(
                src_ref=x.zface.at[phase] if merged else source(port),
                dst_ref=x.fland.at[phase, opposite],
                send_sem=x.fsend_sem.at[phase, port],
                recv_sem=x.frecv_sem.at[phase, opposite],
                device_id=(target,),
                device_id_type=MESH,
            ))
        return copies

    def start_faces(self, phase, ref):
        x = self.x
        if self.merged:
            lower, upper = self.span(FACES - 2), self.span(FACES - 1)
            x.zface[phase] = jnp.where(x.shared[:, lower] > 0.0, ref[:, lower], ref[:, upper])
        copies = self.face_copies(phase, lambda face: ref.at[:, self.span(face)])
        for copy in copies:
            copy.start()
        return copies

    def far_face(self, phase, face):
        return self.x.fland[phase, min(face, self.ports - 1)] * self.x.shared[:, self.span(face)]

    def all_copy(self, phase, source, landing, target):
        x = self.x
        return pltpu.make_async_remote_copy(
            src_ref=source, dst_ref=landing, send_sem=x.tsend_sem.at[phase],
            recv_sem=x.trecv_sem.at[phase], device_id=(target,), device_id_type=MESH,
        )

    def send_all(self, phase, tile):
        x = self.x
        lane = lax.broadcasted_iota(jnp.int32, (ROWS // 2, LANES), 1)
        packed = jnp.where(lane < HALF, tile[: ROWS // 2], pltpu.roll(tile, HALF, 1)[ROWS // 2 :])
        x.tsend[phase] = packed
        source, landing = x.tsend.at[phase], x.tland.at[phase, self.me]
        self.others(lambda target: self.all_copy(phase, source, landing, target).start())
        x.tland[phase, self.me] = packed

    def wait_all(self, phase):
        part = self.x.tland.at[phase, pl.ds(0, self.slots - 1)]
        whole = self.all_copy(phase, part, part, lax.rem(self.me + 1, self.slots))
        whole.wait_recv()
        whole.wait_send()


    def own_inverse(self, block):
        lane = lax.broadcasted_iota(jnp.int32, (1, LANES), 1)
        sub = lax.broadcasted_iota(jnp.int32, (ROWS, 1), 0)
        for k in range(MODES):
            here = lane == k
            row, column = block[k : k + 1, :], block[:, k : k + 1]
            scale = 1.0 / block[k : k + 1, k : k + 1]
            use = row * scale
            fresh = jnp.where(here, column * scale, block - column * use)
            block = jnp.where(sub == k, jnp.where(here, -scale, use), fresh)
        return -block

    def own_block(self):
        x = self.x
        lane = lax.broadcasted_iota(jnp.int32, (1, LANES), 1)
        own = jnp.zeros((ROWS, LANES), jnp.float32)
        for b in range(MODES):
            own = jnp.where(lane == b, row_sum(x.modes[...] * x.modes[b : b + 1, :]), own)
        x.own[0], x.own[1] = own, self.own_inverse(own)
        x.small[...] = jnp.zeros((ROWS, LANES), jnp.float32)
        for a in range(MODES):
            x.small[a : a + 1, : self.loads] = x.goal[a]

    def coarse_row(self):
        x = self.x
        lane = lax.broadcasted_iota(jnp.int32, (1, LANES), 1)
        own, inverse = x.own[0], x.own[1]
        far = jnp.zeros((ROWS, LANES), jnp.float32)
        for face in range(FACES):
            span = self.span(face)
            for b in range(MODES):
                value = row_sum(x.modes[:, span] * x.far[b : b + 1, span])
                far = jnp.where(lane == (face + 1) * ROWS + b, -value, far)
        scaled = inverse
        for b in range(MODES):
            scaled += inverse[:, b : b + 1] * far[b : b + 1, :]
        apart = sum((self.me == slot).astype(jnp.int32) for slot in self.apart)
        goal = pltpu.roll(x.small[...], HALF - ROWS, 1)
        return jnp.where(apart > 0, scaled, far + own) + goal

    def spread_rows(self):
        x, n, phase = self.x, self.slots, ROUNDS
        for slot in range(n):
            packed = x.tland[phase, slot]
            tile = jnp.concatenate([packed, pltpu.roll(packed, HALF, 1)], axis=0)
            tiles = [None] * (self.width // LANES)
            for g, by in enumerate(BLOCK_STEPS):
                target = (slot + by) % n
                place = self.lane_of[target]
                for index in {place // LANES, (place + MODES - 1) // LANES}:
                    table = x.table[0:1, index * LANES : (index + 1) * LANES]
                    moved = pltpu.roll(tile, (place - g * ROWS) % LANES, 1)
                    part = jnp.where(table == target, moved, 0.0)
                    tiles[index] = part if tiles[index] is None else tiles[index] + part
            for index, part in enumerate(tiles):
                if part is None:
                    part = jnp.zeros((ROWS, LANES), jnp.float32)
                x.qrows[slot, :, index * LANES : (index + 1) * LANES] = part

    def eliminate(self):
        out = self.x.dense
        lane = lax.broadcasted_iota(jnp.int32, (1, self.first), 1)
        modes = range(MODES)

        def body(step, carry):
            k = step * MODES
            at = [lane == k + a for a in modes]
            rows = [out[pl.ds(k + a, 1), :] for a in modes]
            block = [[None] * MODES for a in modes]
            for a in modes:
                for b in range(a, MODES):
                    block[a][b] = row_sum(jnp.where(at[b], rows[a], 0.0))
                    block[b][a] = block[a][b]
            for c in modes:
                scale = 1.0 / block[c][c]
                column = [block[a][c] for a in modes]
                use = [column[a] * scale for a in modes]
                for a in modes:
                    for b in range(a, MODES):
                        if a == c and b == c:
                            fresh = -scale
                        elif b == c:
                            fresh = use[a]
                        elif a == c:
                            fresh = use[b]
                        else:
                            fresh = block[a][b] - column[a] * use[b]
                        block[a][b] = block[b][a] = fresh
            uses = []
            for a in modes:
                use = -block[a][0] * rows[0]
                for b in range(1, MODES):
                    use -= block[a][b] * rows[b]
                for b in modes:
                    use = jnp.where(at[b], block[a][b], use)
                uses.append(use)
            whole = out[...]
            fresh = jnp.where((lane >= k) & (lane < k + MODES), 0.0, whole)
            for a in modes:
                fresh -= row_sum(jnp.where(at[a], whole, 0.0)) * uses[a]
            out[...] = fresh
            for a in modes:
                out[pl.ds(k + a, 1), :] = uses[a]
            return carry

        lax.fori_loop(0, len(self.rest), body, 0)

    def coarse_inverse(self):
        x, n, first, half = self.x, self.slots, self.first, ROWS // 2
        self.spread_rows()
        x.packed[...] = jnp.zeros(x.packed.shape, jnp.float32)
        for slot in range(n):
            at = self.lane_of[slot]
            x.packed[at : at + MODES, :] = x.qrows[slot, :MODES, :]
        x.dense[...] = x.packed[:first, :first] - high_dot(
            x.packed[:first, first:], x.packed[first:, :first]
        )
        with jax.named_scope("eliminate"):
            self.eliminate()
        laneslot, lanemode = x.table[0:1, :], x.table[1:2, :]
        lane = lax.broadcasted_iota(jnp.int32, (1, self.width), 1)
        sub = lax.broadcasted_iota(jnp.int32, (ROWS, 1), 0)
        for slot in range(n):
            unit = jnp.where((laneslot == slot) & (lanemode == sub), 1.0, 0.0)
            if slot in self.apart:
                unit -= jnp.where((lane < first) & (sub < MODES), x.qrows[slot], 0.0)
            x.basis[slot * ROWS : (slot + 1) * ROWS, :] = unit
            x.halves[0, slot * half : (slot + 1) * half, :] = unit[:half]
            x.halves[1, slot * half : (slot + 1) * half, :] = unit[half:]
        chosen = jnp.concatenate([
            x.basis[pl.ds(pl.multiple_of(lax.rem(self.me + by + n, n) * ROWS, ROWS), ROWS), :]
            for by in BLOCK_STEPS
        ], axis=0)
        solved = jnp.concatenate([
            -high_dot(chosen[:, :first], x.dense[...]),
            high_dot(chosen[:, first:], x.packed[first:, first:]),
        ], axis=1)
        rows = chosen.shape[0]
        x.picks[:rows] = high_dot(solved, x.halves[0], NT)
        x.picks[rows:] = high_dot(solved, x.halves[1], NT)

    def coarse_columns(self, values, left, right):
        found = high_dot(self.x.picks[...], values)
        rows = ROWS * (FACES + 1)
        return [
            [row_sum(found[at : at + 1] * left + found[rows + at : rows + at + 1] * right)
             for at in range(g * ROWS, g * ROWS + MODES)]
            for g in range(FACES + 1)
        ]

    def rigid_part(self, z, face):
        x, span = self.x, self.span(face)
        total = jnp.zeros((ROWS, self.cap), jnp.float32)
        for a in range(MODES):
            total += z[0][a] * x.modes[a : a + 1, span]
            total -= z[face + 1][a] * x.far[a : a + 1, span]
        return total


    def rigid_product(self, z, at):
        total = z[0][0] * self.x.yrigid[0:1, at]
        for g in range(FACES + 1):
            for a in range(MODES):
                if g or a:
                    total += z[g][a] * self.x.yrigid[g * ROWS + a : g * ROWS + a + 1, at]
        return total

    def product(self, rows, out):
        x, wide = self.x, WIDE

        def body(block, carry):
            at = pl.ds(pl.multiple_of(block * wide, wide), wide)
            both = jnp.dot(
                x.stack[: 2 * rows, :], x.dual[:, at], preferred_element_type=jnp.float32
            )
            out[:, at] = both[:rows] + both[rows:]
            return carry

        lax.fori_loop(0, self.nmax // wide, body, 0)

    def stack_vector(self, at, block):
        parts = [piece.astype(jnp.float32) for piece in split(block, 2)]
        self.x.stack[: 2 * ROWS, at] = jnp.concatenate(parts, axis=0).astype(jnp.bfloat16)

    def rigid_products(self):
        x = self.x

        def keep(at, block):
            x.dofs[:, at] = block

        self.to_dof(x.far, 3, keep)
        sub = lax.broadcasted_iota(jnp.int32, (ROWS, LOW), 0)
        for block in range(self.highs):
            at = slice(block * LOW, (block + 1) * LOW)
            codes = x.codes[:, at]
            own = jnp.where((codes >= 0) & (sub < MODES), x.pad[:, at], 0.0)
            own = [piece.astype(jnp.float32) for piece in split(own, 2)]
            far = [piece.astype(jnp.float32) for piece in split(-x.dofs[:, at], 2)]
            rows = []
            for index in range(2):
                rows.append(own[index])
                for face in range(FACES):
                    here = (codes >= face * self.cap) & (codes < (face + 1) * self.cap)
                    rows.append(jnp.where(here, far[index], 0.0))
            x.stack[: len(rows) * ROWS, at] = jnp.concatenate(rows, axis=0).astype(jnp.bfloat16)
        self.product(ROWS * (FACES + 1), x.yrigid)

    def contributions(self, ref, scalars):
        x = self.x
        lane = lax.broadcasted_iota(jnp.int32, (ROWS, LANES), 1)
        sub = lax.broadcasted_iota(jnp.int32, (ROWS, LANES), 0)
        out = jnp.zeros((ROWS, LANES), jnp.float32)
        for load in range(self.loads):
            own = jnp.zeros((ROWS, self.cap), jnp.float32)
            for face in range(FACES):
                span = self.span(face)
                row = ref[load : load + 1, span]
                own += x.modes[:, span] * row
                other = row_sum(x.far[:, span] * row)
                out = jnp.where(lane == load * ROWS + face + 1, -other, out)
            out = jnp.where(lane == load * ROWS, row_sum(own), out)
        if scalars:
            spread = jnp.zeros((ROWS, LANES), jnp.float32)
            for index, value in enumerate(scalars):
                spread = jnp.where(lane == sub * ROWS + index, value, spread)
            out = jnp.where(sub == MODES, jnp.sum(spread, axis=0, keepdims=True), out)
        return out

    def collect(self, phase):
        x, n, half = self.x, self.slots, ROWS // 2
        group = jnp.bitwise_and(lax.broadcasted_iota(jnp.int32, (half, LANES), 1), ROWS - 1)
        total = x.tland[phase, 0]
        for slot in range(1, n):
            total = total + x.tland[phase, slot]
        for slot in range(n):
            value = x.tland[phase, slot]
            for face in range(FACES):
                sender = (slot - FACE_STEPS[face]) % n
                value = jnp.where(group == face + 1, x.tland[phase, sender], value)
            x.merged[slot * half : (slot + 1) * half, :] = value
        lane = lax.broadcasted_iota(jnp.int32, (ROWS, LANES), 1)
        sub = lax.broadcasted_iota(jnp.int32, (ROWS, LANES), 0)
        left = jnp.where(jnp.right_shift(lane, 3) == sub, 1.0, 0.0)
        right = jnp.where(jnp.right_shift(lane, 3) == sub + ROWS, 1.0, 0.0)
        z = self.coarse_columns(x.merged[...], left, right)
        row = total[MODES - half : MODES - half + 1, :]
        sums = [
            row_sum(jnp.where(lane == HALF + sub * ROWS + i, row, 0.0)) for i in range(4)
        ]
        return z, sums

    def exchange(self, phase, scalars, more):
        x = self.x

        def keep(at, block):
            x.y[phase, :, at] = block

        with jax.named_scope("to_face"):
            self.to_face(x.yw, 2, keep)
        with jax.named_scope("contrib"):
            ref = x.y.at[phase]
            copies = self.start_faces(phase + 1, ref)
            self.send_all(phase, self.contributions(ref, scalars(ref)))
        with jax.named_scope("f_wait"):
            for copy in copies:
                copy.wait()
        for face in range(FACES):
            span = self.span(face)
            x.a[:, span] = ref[:, span] - self.far_face(phase + 1, face)
        if more:
            with jax.named_scope("a_dof"):
                self.to_dof(x.a, 2, self.stack_vector)
            with jax.named_scope("dual_dot"):
                self.product(ROWS, x.yfresh)
        with jax.named_scope("t_wait"):
            self.wait_all(phase)
        with jax.named_scope("collect"):
            return self.collect(phase)


    def run(self, sizes_ref, neighbours_ref, counts_ref, map_ref, modes_ref, local_ref,
            goal_ref, table_ref, dual_ref, mult_out, resid_out, x):
        self.x = x
        self.me = lax.axis_index("dev")
        n, f32 = self.slots, jnp.float32
        inputs = (
            (map_ref, x.map), (counts_ref, x.counts), (neighbours_ref, x.links),
            (modes_ref, x.raw), (local_ref, x.local), (goal_ref, x.goal), (table_ref, x.table),
        )
        inputs = [
            pltpu.make_async_copy(source, target, x.in_sem.at[index])
            for index, (source, target) in enumerate(inputs)
        ]
        for copy in inputs:
            copy.start()
        barrier = pltpu.get_barrier_semaphore()
        self.others(lambda target: pl.semaphore_signal(
            barrier, inc=1, device_id=(target,), device_id_type=MESH
        ))

        with jax.named_scope("inputs"):
            for copy in inputs:
                copy.wait()
            loads = []
            for block in range(self.highs):
                at = pl.ds(block * LOW, LOW)
                copy = pltpu.make_async_copy(
                    dual_ref.at[0, at, :], x.dual.at[at, :], x.dual_sem.at[block]
                )
                copy.start()
                loads.append(copy)
        with jax.named_scope("codes"):
            columns = lax.broadcasted_iota(jnp.int32, (1, self.nmax), 1)
            x.codes[...] = jnp.where(columns < sizes_ref[0], x.map[...], -1)
            self.spread_low(x.codes, x.onehot)
            place = lax.broadcasted_iota(jnp.int32, (1, self.cap), 1)
            for face in range(FACES):
                counted = jnp.where(place < x.counts[0, face], 1.0, 0.0)
                both = jnp.where(x.links[0, face] >= 0, counted, jnp.zeros_like(counted))
                x.counted[:, self.span(face)] = counted
                x.shared[:, self.span(face)] = both
                x.weights[:, self.span(face)] = counted - 0.5 * both
            for a in range(MODES):
                x.pad[a : a + 1, :] = x.raw[a]
            x.pad[MODES : MODES + 1, :] = jnp.right_shift(columns, 8).astype(f32)
            x.pad[MODES + 1 :, :] = jnp.bitwise_and(columns, LOW - 1).astype(f32)
        with jax.named_scope("modes_face"):
            self.scatter_modes()
        with jax.named_scope("barrier_wait"):
            pl.semaphore_wait(barrier, n - 1)
            copies = self.start_faces(0, x.modes)
        with jax.named_scope("places"):
            self.own_block()
            self.spread_low(x.places, x.unhot)
        with jax.named_scope("modes_wait"):
            for copy in copies:
                copy.wait()
        with jax.named_scope("coarse_row"):
            for face in range(FACES):
                x.far[:, self.span(face)] = self.far_face(0, face)
            self.send_all(ROUNDS, self.coarse_row())
        with jax.named_scope("dual_wait"):
            for copy in loads:
                copy.wait()
        with jax.named_scope("rigid_products"):
            self.rigid_products()
        with jax.named_scope("q_wait"):
            self.wait_all(ROUNDS)
        with jax.named_scope("coarse_inverse"):
            self.coarse_inverse()

        for slot in range(n):
            x.merged[slot * ROWS // 2 : (slot + 1) * ROWS // 2, :] = x.tland[ROUNDS, slot]
        lane = lax.broadcasted_iota(jnp.int32, (ROWS, LANES), 1)
        sub = lax.broadcasted_iota(jnp.int32, (ROWS, LANES), 0)
        left = jnp.where(lane == sub + (HALF - ROWS), 1.0, 0.0)
        right = jnp.where(lane == sub + (LANES - ROWS), 1.0, 0.0)
        z = self.coarse_columns(x.merged[...], left, right)
        for face in range(FACES):
            span = self.span(face)
            x.m[:, span] = self.rigid_part(z, face)
            local = jnp.where(x.codes[:, span] >= 0, x.local[0, :, span], 0.0)
            x.yw[:, span] = local - self.rigid_product(z, span)

        z, _ = self.exchange(0, lambda ref: None, True)
        for face in range(FACES):
            span = self.span(face)
            x.w[:, span] = x.a[:, span] - self.rigid_part(z, face)
            x.yw[:, span] = x.yfresh[:, span] - self.rigid_product(z, span)

        for phase in range(1, ROUNDS):
            def scalars(ref):
                w, y = x.w[...], ref[...]
                weighted = w * x.weights[...]
                zero = jnp.zeros((ROWS, 1), f32)
                return [
                    row_sum(weighted * w),
                    row_sum(w * y),
                    row_sum(weighted * x.q[...]) if phase > 1 else zero,
                    row_sum(x.d[...] * y) if phase > 1 else zero,
                ]

            z, (rho, wa, wq, da) = self.exchange(phase, scalars, phase < ITERS)
            if phase > 1:
                beta = rho / rho_old
                curve = wa + beta * (wq + da) + beta * beta * curve
            else:
                curve = wa
            step = rho / curve
            rho_old = rho
            for face in range(FACES):
                span = self.span(face)
                applied = x.a[:, span]
                d, q, s = x.w[:, span], applied, applied - self.rigid_part(z, face)
                if phase > 1:
                    d += beta * x.d[:, span]
                    s += beta * x.s[:, span]
                x.m[:, span] += step * d
                x.w[:, span] -= step * s
                if phase < ITERS:
                    if phase > 1:
                        q += beta * x.q[:, span]
                    x.d[:, span], x.q[:, span], x.s[:, span] = d, q, s
                    ys = x.yfresh[:, span] - self.rigid_product(z, span)
                    if phase > 1:
                        ys += beta * x.ys[:, span]
                    x.ys[:, span] = ys
                    x.yw[:, span] -= step * ys

        with jax.named_scope("final"):
            for ref, out in ((x.m, mult_out), (x.w, resid_out)):
                def put(at, block, out=out):
                    out[0, :, at] = block
                self.to_dof(ref, 3, put)


class Refs:
    def __init__(self, names, refs):
        self.__dict__.update(zip(names, refs))


def per_device(
    dual_blocks, rigid_modes, dual_local, coarse_rhs, iface_sizes, neighbours, shared_counts,
    iface_map, owner,
):
    slots = lax.axis_size("dev")
    loads, nmax = dual_local.shape[1:]
    solver = Solver(slots, loads, nmax, nmax // FACES)
    scratch = solver.scratch()
    names = list(scratch)

    def kernel(*refs):
        solver.run(*refs[:11], Refs(names, refs[11:]))

    laneslot, lanemode = [-1] * solver.width, [-1] * solver.width
    for slot, at in solver.lane_of.items():
        for mode in range(MODES):
            laneslot[at + mode], lanemode[at + mode] = slot, mode
    table = jnp.array([laneslot, lanemode] + [[0] * solver.width] * 6, jnp.int32)
    vmem, smem = pl.BlockSpec(memory_space=pltpu.VMEM), pl.BlockSpec(memory_space=pltpu.SMEM)
    result = jax.ShapeDtypeStruct((1, loads, nmax), jnp.float32)
    solved = pl.pallas_call(
        kernel,
        out_shape=(pltpu.VMEM(result.shape, jnp.float32),) * 2,
        in_specs=[smem] + [pl.BlockSpec(memory_space=pltpu.HBM)] * 8,
        out_specs=(vmem, vmem),
        scratch_shapes=list(scratch.values()),
        compiler_params=pltpu.CompilerParams(
            collective_id=0, has_side_effects=True, vmem_limit_bytes=48 * 2**20
        ),
    )(iface_sizes, *[
        pltpu.with_memory_space_constraint(item, pltpu.HBM) for item in (
            neighbours, shared_counts, iface_map, rigid_modes.transpose(1, 0, 2), dual_local,
            coarse_rhs.transpose(1, 0, 2), table, dual_blocks,
        )
    ])

    def hand_over(*refs):
        copies = [pltpu.make_async_copy(refs[i], refs[2 + i], refs[4].at[i]) for i in range(2)]
        for copy in copies:
            copy.start()
        for copy in copies:
            copy.wait()

    return pl.pallas_call(
        hand_over,
        out_shape=(result, result),
        in_specs=[vmem] * 2,
        out_specs=(pl.BlockSpec(memory_space=pltpu.HBM),) * 2,
        scratch_shapes=[pltpu.SemaphoreType.DMA((2,))],
    )(*[pltpu.with_memory_space_constraint(item, pltpu.VMEM) for item in solved])


def solution(mesh):
    return jax.shard_map(
        per_device,
        mesh=mesh,
        in_specs=(
            P("dev", None, None),
            P("dev", None, None),
            P("dev", None, None),
            P("dev", None, None),
            P("dev"),
            P("dev", None),
            P("dev", None),
            P("dev", None),
            P(),
        ),
        out_specs=(P("dev", None, None), P("dev", None, None)),
        check_vma=False,
    )
```

time: 85.5 us -> 58.1 us (0.68)
  Pallas kernels: 77.9 us -> 56.4 us
  local copies, waits for them, and re-layouts: 5.98 us -> 0 us
    pallas_call x1 -> x2, Pallas kernels: 77.9 us -> 56.4 us  [the longest x1 55.7 us: per_device(): pl.pallas_call(kernel, out_shape=(pltpu.VMEM(result.shape, jnp.float32),)...]
    unnamed x4 -> x0, local copies, waits for them, and re-layouts: 5.31 us -> none
where the time goes in v2:
time: 58.1 us; the launch traced here: 57.8 us
  Pallas kernels  56.4 us (97%)
  between operations  1.45 us (2%)
    pallas_call x1, Pallas kernels, per_device(): pl.pallas_call(kernel, out_shape=(pltpu.VMEM(result.shape, jnp.float32),)...  55.7 us

profile of v2, /device:TPU:0, one launch (start us, length us, event | category | flops | bytes accessed | tf_op | source)
XLA Modules:
  0.0 57.8 jit_solution(12776381314720222447)
XLA Ops:
  1.3 55.7 %shard_map.104 = (f32[1,8,3072]{2,1,0:T(8,128)S(1)}, f32[1,8,3072]{2,1,0:T(8,128)S(1)}) custom-call(s32[1]{0:T(128)S(6)} %copy.11.refs_0_, s32[1,6]{1,0:T(1,128)} %refs_1_.1, s32[1,6]{1,0:T(1,128)} %refs_2_.1, s32[1,3072]{1,0:T(1,128)} %refs_3_.1, f32[6,1,3072]{2,1,0:T(1,128)} %bitcast.2, f32[1,8,3072]{2,1,0:T(8,128)} %refs_5_.1, f32[6,1,8]{2,1,0:T(1,128)} %bitcast.3, ...), custom_call_target="tpu_custom_call" | custom-call | tf_op jit(solution)/shard_map/pallas_call | solution.py:698
  57.0 0.7 %shard_map.105 = (f32[1,8,3072]{2,1,0:T(8,128)}, f32[1,8,3072]{2,1,0:T(8,128)}) custom-call(f32[1,8,3072]{2,1,0:T(8,128)S(1)} %get-tuple-element.4.refs_0_, f32[1,8,3072]{2,1,0:T(8,128)S(1)} %get-tuple-element.5.refs_1_), custom_call_target="tpu_custom_call" | custom-call | tf_op jit(solution)/shard_map/pallas_call | solution.py:721

commit v3 on v2

--- a/solution.py
+++ b/solution.py
@@ -14,6 +14,7 @@
 LANES = 128
 HALF = 64
 WIDE = 1536
+CUT = 2048
 LOW = 256
 ROWS = 8
 FACE_STEPS = (-1, 1, -4, 4, -16, 16)
@@ -78,7 +79,7 @@
         return dict(
             dual=pltpu.VMEM((nmax, nmax), jnp.bfloat16),
             onehot=pltpu.VMEM((LOW, nmax), jnp.bfloat16),
-            stack=pltpu.VMEM((3 * ROWS * self.highs, nmax), jnp.bfloat16),
+            stack=pltpu.VMEM((2 * ROWS * self.highs, nmax), jnp.bfloat16),
             codes=pltpu.VMEM((1, nmax), jnp.int32),
             places=pltpu.VMEM((1, nmax), jnp.int32),
             unhot=pltpu.VMEM((LOW, nmax), jnp.bfloat16),
@@ -141,7 +142,7 @@
         lax.fori_loop(0, self.nmax // LANES, body, 0)
 
     def scatter_modes(self):
-        x, rows, parts = self.x, ROWS * self.highs, 3
+        x, rows, parts = self.x, ROWS * self.highs, 2
 
         def body(block, carry):
             at = pl.ds(pl.multiple_of(block * LOW, LOW), LOW)
@@ -156,9 +157,9 @@
 
         lax.fori_loop(0, self.highs, body, 0)
         found = lax.dot_general(
-            x.stack[...], x.onehot[...], NT, preferred_element_type=jnp.float32
+            x.stack[: parts * rows], x.onehot[...], NT, preferred_element_type=jnp.float32
         )
-        total = found[:rows] + found[rows : 2 * rows] + found[2 * rows :]
+        total = found[:rows] + found[rows:]
         sub = lax.broadcasted_iota(jnp.int32, (ROWS, LOW), 0)
         for h in range(self.highs):
             at = slice(h * LOW, (h + 1) * LOW)
@@ -421,18 +422,12 @@
                     total += z[g][a] * self.x.yrigid[g * ROWS + a : g * ROWS + a + 1, at]
         return total
 
-    def product(self, rows, out):
-        x, wide = self.x, WIDE
-
-        def body(block, carry):
-            at = pl.ds(pl.multiple_of(block * wide, wide), wide)
-            both = jnp.dot(
-                x.stack[: 2 * rows, :], x.dual[:, at], preferred_element_type=jnp.float32
-            )
-            out[:, at] = both[:rows] + both[rows:]
-            return carry
-
-        lax.fori_loop(0, self.nmax // wide, body, 0)
+    def product(self, rows, out, at):
+        x = self.x
+        both = jnp.dot(
+            x.stack[: 2 * rows, :], x.dual[:, at], preferred_element_type=jnp.float32
+        )
+        out[:, at] = both[:rows] + both[rows:]
 
     def stack_vector(self, at, block):
         parts = [piece.astype(jnp.float32) for piece in split(block, 2)]
@@ -444,7 +439,7 @@
         def keep(at, block):
             x.dofs[:, at] = block
 
-        self.to_dof(x.far, 3, keep)
+        self.to_dof(x.far, 2, keep)
         sub = lax.broadcasted_iota(jnp.int32, (ROWS, LOW), 0)
         for block in range(self.highs):
             at = slice(block * LOW, (block + 1) * LOW)
@@ -459,7 +454,13 @@
                     here = (codes >= face * self.cap) & (codes < (face + 1) * self.cap)
                     rows.append(jnp.where(here, far[index], 0.0))
             x.stack[: len(rows) * ROWS, at] = jnp.concatenate(rows, axis=0).astype(jnp.bfloat16)
-        self.product(ROWS * (FACES + 1), x.yrigid)
+
+        def body(block, carry):
+            at = pl.ds(pl.multiple_of(block * WIDE, WIDE), WIDE)
+            self.product(ROWS * (FACES + 1), x.yrigid, at)
+            return carry
+
+        lax.fori_loop(0, self.nmax // WIDE, body, 0)
 
     def contributions(self, ref, scalars):
         x = self.x
@@ -513,10 +514,13 @@
 
         with jax.named_scope("to_face"):
             self.to_face(x.yw, 2, keep)
-        with jax.named_scope("contrib"):
-            ref = x.y.at[phase]
+        ref = x.y.at[phase]
+        if more:
             copies = self.start_faces(phase + 1, ref)
             self.send_all(phase, self.contributions(ref, scalars(ref)))
+        else:
+            self.send_all(phase, self.contributions(ref, scalars(ref)))
+            copies = self.start_faces(phase + 1, ref)
         with jax.named_scope("f_wait"):
             for copy in copies:
                 copy.wait()
@@ -527,11 +531,14 @@
             with jax.named_scope("a_dof"):
                 self.to_dof(x.a, 2, self.stack_vector)
             with jax.named_scope("dual_dot"):
-                self.product(ROWS, x.yfresh)
+                self.product(ROWS, x.yfresh, slice(0, CUT))
         with jax.named_scope("t_wait"):
             self.wait_all(phase)
         with jax.named_scope("collect"):
-            return self.collect(phase)
+            found = self.collect(phase)
+            if more:
+                self.product(ROWS, x.yfresh, slice(CUT, self.nmax))
+            return found
 
 
     def run(self, sizes_ref, neighbours_ref, counts_ref, map_ref, modes_ref, local_ref,
@@ -622,6 +629,8 @@
         for face in range(FACES):
             span = self.span(face)
             x.w[:, span] = x.a[:, span] - self.rigid_part(z, face)
+        for face in range(FACES):
+            span = self.span(face)
             x.yw[:, span] = x.yfresh[:, span] - self.rigid_product(z, span)
 
         for phase in range(1, ROUNDS):
@@ -657,6 +666,9 @@
                     if phase > 1:
                         q += beta * x.q[:, span]
                     x.d[:, span], x.q[:, span], x.s[:, span] = d, q, s
+            if phase < ITERS:
+                for face in range(FACES):
+                    span = self.span(face)
                     ys = x.yfresh[:, span] - self.rigid_product(z, span)
                     if phase > 1:
                         ys += beta * x.ys[:, span]
@@ -667,7 +679,7 @@
             for ref, out in ((x.m, mult_out), (x.w, resid_out)):
                 def put(at, block, out=out):
                     out[0, :, at] = block
-                self.to_dof(ref, 3, put)
+                self.to_dof(ref, 2, put)
 
 
 class Refs:

time: 58.1 us -> 55.2 us (0.950)
  Pallas kernels: 56.4 us -> 53.5 us
    pallas_call x1, Pallas kernels: 55.7 us -> 52.8 us  [per_device(): pl.pallas_call(kernel, out_shape=(pltpu.VMEM(result.shape, jnp.float32),)...]
where the time goes in v3:
time: 55.2 us; the launch traced here: 55 us
  Pallas kernels  53.5 us (97%)
  between operations  1.45 us (3%)
    pallas_call x1, Pallas kernels, per_device(): pl.pallas_call(kernel, out_shape=(pltpu.VMEM(result.shape, jnp.float32),)...  52.8 us

profile of v3, /device:TPU:0, one launch (start us, length us, event | category | flops | bytes accessed | tf_op | source)
XLA Modules:
  0.0 55.0 jit_solution(11237138846906407734)
XLA Ops:
  1.3 52.8 %shard_map.104 = (f32[1,8,3072]{2,1,0:T(8,128)S(1)}, f32[1,8,3072]{2,1,0:T(8,128)S(1)}) custom-call(s32[1]{0:T(128)S(6)} %copy.11.refs_0_, s32[1,6]{1,0:T(1,128)} %refs_1_.1, s32[1,6]{1,0:T(1,128)} %refs_2_.1, s32[1,3072]{1,0:T(1,128)} %refs_3_.1, f32[6,1,3072]{2,1,0:T(1,128)} %bitcast.2, f32[1,8,3072]{2,1,0:T(8,128)} %refs_5_.1, f32[6,1,8]{2,1,0:T(1,128)} %bitcast.3, ...), custom_call_target="tpu_custom_call" | custom-call | tf_op jit(solution)/shard_map/pallas_call | solution.py:710
  54.1 0.7 %shard_map.105 = (f32[1,8,3072]{2,1,0:T(8,128)}, f32[1,8,3072]{2,1,0:T(8,128)}) custom-call(f32[1,8,3072]{2,1,0:T(8,128)S(1)} %get-tuple-element.4.refs_0_, f32[1,8,3072]{2,1,0:T(8,128)S(1)} %get-tuple-element.5.refs_1_), custom_call_target="tpu_custom_call" | custom-call | tf_op jit(solution)/shard_map/pallas_call | solution.py:733
